TPU v7x, 32 devices: a 4x4x1 block of a 4x4x8 slice. The times are simulated.
32 devices in a mesh: dp: 1 (over z), tp: 32 (over y, x, core).
Axes of the slice: x: 4, y: 4, z: 1, core: 2. Of those that a mesh axis runs over, the one named last changes fastest.
The devices are a block of a 4x4x8 slice.
Arguments:
- x_saved: bfloat16 [2, 1024, 3072], P('dp')
- h1_saved: bfloat16 [2, 1024, 3072], P('dp')
- grad_y: bfloat16 [2, 1024, 3072], P('dp')
- mean_one: float32 [2, 1024], P('dp')
- rstd_one: float32 [2, 1024], P('dp')
- mean_two: float32 [2, 1024], P('dp')
- rstd_two: float32 [2, 1024], P('dp')
- gain_one: bfloat16 [3072], replicated
- gain_two: bfloat16 [3072], replicated
- w_qkv: bfloat16 [3072, 32, 3, 96], P(None, 'tp')
- w_out: bfloat16 [32, 96, 3072], P('tp')
- w_up: bfloat16 [3072, 12288], P(None, 'tp')
- w_down: bfloat16 [12288, 3072], P('tp')
Outputs:
- output 1: bfloat16 [2, 1024, 3072], P('dp')
- output 2: bfloat16 [3072, 32, 3, 96], P('dp', 'tp')
- output 3: bfloat16 [32, 96, 3072], P(('dp', 'tp'))
- output 4: bfloat16 [3072, 12288], P('dp', 'tp')
- output 5: bfloat16 [12288, 3072], P(('dp', 'tp'))
All inputs are finite; a program needn't handle non-finite values.
Results may differ from a plain program's by a relative error of at most 0.0199183.
Values are sent between devices in bfloat16 or wider.
A program may use at most 768 MiB of HBM per device.

v0:
```python
import math
import jax
import jax.numpy as jnp
from jax import lax
from jax.experimental import pallas as pl
from jax.experimental.pallas import tpu as pltpu
from jax.sharding import PartitionSpec as P
from functools import partial

GELU_C = 0.7978845608028654
GELU_A = 0.044715
F32 = jnp.float32
BF16 = jnp.bfloat16
ANY = pl.ANY
VMEM = pltpu.VMEM
wide_einsum = partial(jnp.einsum, preferred_element_type=F32)


def gelu_tanh(pre_act):
    inner_arg = GELU_C * (pre_act + GELU_A * pre_act * pre_act * pre_act)
    return 0.5 * pre_act * (1.0 + jnp.tanh(inner_arg))


def gelu_slope(pre_act):
    inner_arg = GELU_C * (pre_act + GELU_A * pre_act * pre_act * pre_act)
    tanh_val = jnp.tanh(inner_arg)
    return (0.5 * (1.0 + tanh_val)
            + 0.5 * pre_act * (1.0 - tanh_val * tanh_val) * GELU_C * (1.0 + 3.0 * GELU_A * pre_act * pre_act))


def attention_backward(q_heads, k_heads, v_heads, grad_o, score_scale):
    seq_len = q_heads.shape[1]
    scores = wide_einsum('bqnd,bknd->bnqk', q_heads, k_heads) * score_scale
    causal = jnp.arange(seq_len)[:, None] >= jnp.arange(seq_len)[None, :]
    attn_prob = jax.nn.softmax(jnp.where(causal, scores, -1e30), axis=-1)
    prob_bf16 = attn_prob.astype(BF16)
    attn_out = wide_einsum('bnqk,bknd->bqnd', prob_bf16, v_heads).astype(BF16)
    grad_v = wide_einsum('bnqk,bqnd->bknd', prob_bf16, grad_o).astype(BF16)
    grad_p = wide_einsum('bqnd,bknd->bnqk', grad_o, v_heads)
    row_dot = jnp.sum(attn_prob * grad_p, axis=-1, keepdims=True)
    grad_s = (attn_prob * (grad_p - row_dot) * score_scale).astype(BF16)
    grad_q = wide_einsum('bnqk,bknd->bqnd', grad_s, k_heads).astype(BF16)
    grad_k = wide_einsum('bnqk,bqnd->bknd', grad_s, q_heads).astype(BF16)
    return attn_out, jnp.stack([grad_q, grad_k, grad_v], axis=3)


BLOCK = 512
SEMS = 32
LINK = {'1+': 85e3, '1-': 85e3, '2+': 85e3, '2-': 85e3, 'D': 450e3}
LATENCY = 2.3
TICK = 0.3


class Comm:
    def __init__(self, n, rows, cols):
        self.side = math.isqrt(n // 2)
        assert self.side == 4 and 2 * self.side * self.side == n
        self.rows, self.cols = rows, cols
        self.blk = BLOCK
        self.streams = rows // BLOCK
        self.half = self.blk // 2
        self.l1 = self.half // self.side
        self.l2 = self.l1 // self.side
        self.hw = cols // 2

    N_SCRATCH = 12

    def scratch(self):
        l1, l2, w, hw, ns = self.l1, self.l2, self.cols, self.hw, self.streams
        return [
            VMEM((ns, self.half, w), BF16),
            VMEM((ns, self.half, w), BF16),
            VMEM((ns, 6, l1, hw), BF16),
            VMEM((ns, 6, l2, hw), BF16),
            VMEM((self.rows, w), BF16),
            VMEM((ns, l2, w), BF16),
            VMEM((ns, l2, w), BF16),
            VMEM((self.rows, 128), F32),
            VMEM((self.rows, 128), F32),
            pltpu.SemaphoreType.DMA((ns, SEMS)),
            pltpu.SemaphoreType.DMA((ns, SEMS)),
            pltpu.SemaphoreType.DMA((ns, 8)),
            pltpu.SemaphoreType.REGULAR((ns,)),
        ]

    def bind(self, part, saved, resid, mean, rstd, gain, out, scratch):
        (self.own, self.pair, self.ring1, self.ring2, self.full, self.zrow, self.rrow, self.mu, self.rs,
         self.ssem, self.rsem, self.lsem, self.freed) = scratch
        self.part, self.saved, self.resid, self.gain, self.out = part, saved, resid, gain, out
        self.mean, self.rstd = mean, rstd
        side = self.side
        me = lax.axis_index('tp')
        core = lax.rem(me, 2)
        x = lax.rem(lax.div(me, 2), side)
        y = lax.div(me, 2 * side)
        self.core = core
        self.p1 = x * (1 - core) + y * core
        self.p2 = y * (1 - core) + x * core

        def dev(p1, p2):
            p1, p2 = lax.rem(p1 + side, side), lax.rem(p2 + side, side)
            xx = p1 * (1 - core) + p2 * core
            yy = p2 * (1 - core) + p1 * core
            return (yy * side + xx) * 2 + core

        self.partner = me + 1 - 2 * core
        self.ring_devs = {1: (dev(self.p1 + 1, self.p2), dev(self.p1 - 1, self.p2)),
                          2: (dev(self.p1, self.p2 + 1), dev(self.p1, self.p2 - 1))}
        self.sent = []

    def m(self, j):
        return lax.rem(j + self.side, self.side)

    def ds(self, off, size):
        return pl.ds(pl.multiple_of(off, 16), size)

    def half_rows(self, s, which):
        c = self.core if which == 0 else 1 - self.core
        return self.ds(s * self.blk + c * self.half, self.half)

    def copies(self, s):
        side, l1, l2, hw, w = self.side, self.l1, self.l2, self.hw, self.cols
        c, p1, p2, m, ds = self.core, self.p1, self.p2, self.m, self.ds
        left, right = pl.ds(0, hw), pl.ds(hw, hw)
        own, full = self.own.at[s], self.full
        row0 = s * self.blk
        out = {}
        source = self.full if self.part is None else self.part
        out['pair'] = (0, source.at[self.half_rows(s, 1), :], self.pair.at[s], self.partner)

        def ring(tag, first, base, size, p, bufs, devs):
            plus, minus = devs

            def chunk(j, cols):
                return own.at[ds(base + m(j) * size, size), cols]

            out[tag + 'xp'] = (first + 0, chunk(p + 2, left), bufs.at[s, 0], plus)
            out[tag + 'xm'] = (first + 1, chunk(p + 2, right), bufs.at[s, 1], minus)
            out[tag + 'dp'] = (first + 2, chunk(p + 1, right), bufs.at[s, 2], plus)
            out[tag + 'dm'] = (first + 3, chunk(p - 1, left), bufs.at[s, 3], minus)
            out[tag + 'rp'] = (first + 4, chunk(p + 1, left), bufs.at[s, 4], plus)
            out[tag + 'rm'] = (first + 5, chunk(p - 1, right), bufs.at[s, 5], minus)

        ring('a', 1, 0, l1, p1, self.ring1, self.ring_devs[1])
        ring('b', 7, p1 * l1, l2, p2, self.ring2, self.ring_devs[2])

        def gather(tag, first, base, size, p, devs):
            plus, minus = devs

            def chunk(j, cols):
                return full.at[ds(base + m(j) * size, size), cols]

            every = pl.ds(0, w)
            for name, idx, view, to in (('sp', 0, chunk(p, every), plus), ('sm', 1, chunk(p, every), minus),
                                        ('yp', 2, chunk(p - 1, left), plus), ('ym', 3, chunk(p + 1, right), minus)):
                out[tag + name] = (first + idx, view, view, to)

        half0 = row0 + c * self.half
        gather('c', 13, half0 + p1 * l1, l2, p2, self.ring_devs[2])
        gather('d', 17, half0, l1, p1, self.ring_devs[1])
        for j in range(side):
            view = full.at[ds(half0 + m(p1 + j) * l1, l1), :]
            out['k%d' % j] = (21 + j, view, view, self.partner)
        return out

    def get(self, s, name):
        idx, src, dst, to = self.copies(s)[name]
        return pltpu.make_async_remote_copy(src_ref=src, dst_ref=dst, send_sem=self.ssem.at[s, idx],
                                            recv_sem=self.rsem.at[s, idx], device_id={'tp': to},
                                            device_id_type=pl.DeviceIdType.MESH)

    def start(self, s, *names):
        for name in names:
            self.get(s, name).start()
            self.sent.append((s, name))

    def arrived(self, s, *names):
        for name in names:
            self.get(s, name).wait_recv()

    def mine(self, s):
        return self.ds(s * self.blk + self.core * self.half + self.p1 * self.l1 + self.p2 * self.l2, self.l2)

    def local(self, s, idx):
        if idx == 0:
            src, dst = self.part.at[self.half_rows(s, 0), :], self.own.at[s]
        elif idx == 1:
            src, dst = self.saved.at[self.mine(s), :], self.zrow.at[s]
        elif idx == 2:
            src, dst = self.resid.at[self.mine(s), :], self.rrow.at[s]
        else:
            rows = self.half_rows(s, idx - 4)
            src, dst = self.full.at[rows, :], self.out.at[rows, :]
        return pltpu.make_async_copy(src, dst, self.lsem.at[s, idx])

    def barrier(self):
        sem = pltpu.get_barrier_semaphore()
        peers = (self.partner,) + self.ring_devs[1] + self.ring_devs[2]
        for peer in peers:
            pl.semaphore_signal(sem, inc=1, device_id={'tp': peer}, device_id_type=pl.DeviceIdType.MESH)
        pl.semaphore_wait(sem, len(peers))

    def columns(self):
        per = self.mean.shape[1]
        for src, dst in ((self.mean, self.mu), (self.rstd, self.rs)):
            for i in range(self.rows // 128):
                b, off = divmod(i * 128, per)
                row = src[b:b + 1, off:off + 128]
                dst[pl.ds(i * 128, 128), :] = jnp.transpose(jnp.broadcast_to(row, (128, 128)))

    def begin(self):
        for s in range(self.streams):
            if self.part is not None:
                self.local(s, 0).start()
            self.local(s, 1).start()
            self.local(s, 2).start()
        self.barrier()
        if self.part is not None:
            for s in range(self.streams):
                self.start(s, 'pair')
        self.columns()

    def rs1_start(self, s):
        if self.part is not None:
            self.local(s, 0).wait()
        self.arrived(s, 'pair')
        step = self.l1

        def add(i, carry):
            rows = pl.ds(pl.multiple_of(i * step, step), step)
            self.own[s, rows, :] = (self.own[s, rows, :].astype(F32) + self.pair[s, rows, :].astype(F32)).astype(BF16)
            return carry

        lax.fori_loop(0, self.half // step, add, 0)
        self.start(s, 'axp', 'axm', 'adp', 'adm')
        if self.part is None:
            self.get(s, 'pair').wait_send()
            pl.semaphore_signal(self.freed.at[s], inc=1, device_id={'tp': self.partner},
                                device_id_type=pl.DeviceIdType.MESH)

    def relay(self, s, tag, bufs, base, size, p):
        for buf, j, col0, got, nxt in ((0, p + 1, 0, 'xp', 'rp'), (1, p - 1, self.hw, 'xm', 'rm')):
            self.arrived(s, tag + got)
            rows = self.ds(base + self.m(j) * size, size)
            cols = pl.ds(col0, self.hw)
            self.own[s, rows, cols] = (self.own[s, rows, cols].astype(F32) + bufs[s, buf].astype(F32)).astype(BF16)
            self.start(s, tag + nxt)

    def final(self, s, tag, bufs, base, size, p):
        self.arrived(s, tag + 'rp', tag + 'dm', tag + 'rm', tag + 'dp')
        rows = self.ds(base + p * size, size)
        sums = []
        for col0, one, two in ((0, 4, 3), (self.hw, 5, 2)):
            sums.append(self.own[s, rows, pl.ds(col0, self.hw)].astype(F32)
                        + bufs[s, one].astype(F32) + bufs[s, two].astype(F32))
        return rows, sums

    def rs1_relay(self, s):
        self.relay(s, 'a', self.ring1, 0, self.l1, self.p1)

    def rs2_start(self, s):
        rows, sums = self.final(s, 'a', self.ring1, 0, self.l1, self.p1)
        for k in range(2):
            self.own[s, rows, pl.ds(k * self.hw, self.hw)] = sums[k].astype(BF16)
        self.start(s, 'bxp', 'bxm', 'bdp', 'bdm')

    def rs2_relay(self, s):
        self.relay(s, 'b', self.ring2, self.p1 * self.l1, self.l2, self.p2)

    def norm_gather(self, s):
        _, sums = self.final(s, 'b', self.ring2, self.p1 * self.l1, self.l2, self.p2)
        self.local(s, 1).wait()
        self.local(s, 2).wait()
        mine = self.mine(s)
        mu = self.mu[mine, 0:1]
        r = self.rs[mine, 0:1]
        us, xs = [], []
        for k in range(2):
            cols = pl.ds(k * self.hw, self.hw)
            us.append(sums[k] * self.gain[:, cols].astype(F32))
            xs.append((self.zrow[s, :, cols].astype(F32) - mu) * r)
        inv = 1.0 / self.cols
        mean_u = (jnp.sum(us[0], axis=-1, keepdims=True) + jnp.sum(us[1], axis=-1, keepdims=True)) * inv
        mean_c = (jnp.sum(us[0] * xs[0], axis=-1, keepdims=True)
                  + jnp.sum(us[1] * xs[1], axis=-1, keepdims=True)) * inv
        for k in range(2):
            cols = pl.ds(k * self.hw, self.hw)
            grad = self.rrow[s, :, cols].astype(F32) + r * (us[k] - mean_u - xs[k] * mean_c)
            self.full[mine, cols] = grad.astype(BF16)
        self.start(s, 'csp', 'csm')

    def ag2_relay(self, s):
        self.arrived(s, 'csp')
        self.start(s, 'cyp')
        self.arrived(s, 'csm')
        self.start(s, 'cym')

    def ag1_start(self, s):
        self.arrived(s, 'cyp', 'cym')
        if self.part is None:
            pl.semaphore_wait(self.freed.at[s], 1)
        self.start(s, 'dsp', 'dsm', 'k0')

    def ag1_relay(self, s):
        self.arrived(s, 'dsp')
        self.start(s, 'dyp')
        self.arrived(s, 'dsm')
        self.start(s, 'dym', 'k3', 'k1')

    def ag1_final(self, s):
        self.arrived(s, 'dyp', 'dym')
        self.start(s, 'k2')
        self.local(s, 4).start()

    def finish(self, s):
        self.arrived(s, 'k0', 'k1', 'k2', 'k3')
        self.local(s, 5).start()

    def end(self):
        for s, name in self.sent:
            if name != 'pair' or self.part is not None:
                self.get(s, name).wait_send()
        for s in range(self.streams):
            self.local(s, 4).wait()
            self.local(s, 5).wait()

    def stages(self):
        x1, x2 = self.l1 * self.hw * 2, self.l2 * self.hw * 2
        return [
            ('rs1_start', ['pair', 'own'], [('axp', '1+', x1), ('axm', '1-', x1), ('adp', '1+', x1), ('adm', '1-', x1)]),
            ('rs1_relay', ['axp', 'axm'], [('arp', '1+', x1), ('arm', '1-', x1)]),
            ('rs2_start', ['arp', 'arm', 'adp', 'adm'],
             [('bxp', '2+', x2), ('bxm', '2-', x2), ('bdp', '2+', x2), ('bdm', '2-', x2)]),
            ('rs2_relay', ['bxp', 'bxm'], [('brp', '2+', x2), ('brm', '2-', x2)]),
            ('norm_gather', ['brp', 'brm', 'bdp', 'bdm'], [('csp', '2+', 2 * x2), ('csm', '2-', 2 * x2)]),
            ('ag2_relay', ['csp', 'csm'], [('cyp', '2+', x2), ('cym', '2-', x2)]),
            ('ag1_start', ['cyp', 'cym'], [('dsp', '1+', 2 * x1), ('dsm', '1-', 2 * x1), ('k0', 'D', 2 * x1)]),
            ('ag1_relay', ['dsp', 'dsm'], [('dyp', '1+', x1), ('dym', '1-', x1), ('k3', 'D', 2 * x1), ('k1', 'D', 2 * x1)]),
            ('ag1_final', ['dyp', 'dym'], [('k2', 'D', 2 * x1)]),
            ('finish', ['k0', 'k1', 'k2', 'k3'], []),
        ]

    def plan(self, points):
        stages = self.stages()
        pair_bytes = self.half * self.cols * 2
        free = dict.fromkeys(LINK, 0.0)
        done = {}
        at = [0] * self.streams
        now = 0.0

        def push(s, name, link, size):
            free[link] = max(free[link], now) + size / LINK[link]
            done[s, name] = free[link] + LATENCY

        def ready(s):
            if at[s] >= len(stages):
                return math.inf
            return max(done.get((s, need), math.inf) for need in stages[at[s]][1])

        plans = []
        for i, (cost, gives) in enumerate(points):
            now += cost
            todo = []
            for s, what in gives:
                if what == 'pair':
                    push(s, 'pair', 'D', pair_bytes)
                    if self.part_given is False:
                        todo.append(('send_pair', s))
                else:
                    done[s, 'own'] = now
            last = i == len(points) - 1
            while True:
                s = min(range(self.streams), key=ready)
                t = ready(s)
                if t == math.inf or (t > now and not last):
                    break
                now = max(now, t) + TICK
                name, _, sends = stages[at[s]]
                for copy, link, size in sends:
                    push(s, copy, link, size)
                at[s] += 1
                todo.append((name, s))
            plans.append(todo)
        assert all(a == len(stages) for a in at)
        self.estimate = now
        return plans

    def send_pair(self, s):
        self.start(s, 'pair')

    part_given = False


VMEM_LIMIT = 64 * 1024 * 1024 - 64 * 1024


def reduce_norm_gather(n, part, saved, resid, mean, rstd, gain, cid):
    rows, cols = part.shape
    comm = Comm(n, rows, cols)
    comm.part_given = True
    plans = comm.plan([(3.0, [(s, w) for s in range(comm.streams) for w in ('pair', 'own')])])

    def kernel(part_ref, saved_ref, resid_ref, mean_ref, rstd_ref, gain_ref, out_ref, *scratch):
        comm.bind(part_ref, saved_ref, resid_ref, mean_ref, rstd_ref, gain_ref, out_ref, scratch)
        comm.begin()
        for name, s in plans[0]:
            getattr(comm, name)(s)
        comm.end()

    return pl.pallas_call(
        kernel,
        out_shape=jax.ShapeDtypeStruct((rows, cols), BF16),
        in_specs=[pl.BlockSpec(memory_space=ANY)] * 3 + [pl.BlockSpec(memory_space=VMEM)] * 3,
        out_specs=pl.BlockSpec(memory_space=ANY),
        scratch_shapes=comm.scratch(),
        compiler_params=pltpu.CompilerParams(collective_id=cid, has_side_effects=True, vmem_limit_bytes=VMEM_LIMIT),
        name='sum_norm_gather_%d' % cid,
    )(part, saved, resid, mean, rstd, gain)


def dot(a, b, ca=1, cb=0):
    return lax.dot_general(a, b, (((ca,), (cb,)), ((), ())), preferred_element_type=F32)


def mlp_stage(n, h1, dy, mean, rstd, gain, w_up, w_down, cid):
    rows, cols = h1.shape
    ffn = w_up.shape[1]
    comm = Comm(n, rows, cols)
    tile = comm.half
    n_tiles = rows // tile
    cb = 256
    n_cols = cols // cb
    grid = n_tiles + n_cols
    points = []
    for i in range(n_tiles):
        points += [(1.6, []), (1.2, []), (1.2, [(i // 2, 'pair' if i % 2 == 0 else 'own')])]
    for i in range(n_cols):
        points += [(0.6, []), (0.8, []), (0.8, [])]
    plans = comm.plan(points)

    def kernel(h1_tile, dy_tile, h1_col, dy_col, w1, w2, mean_ref, rstd_ref, gain_ref, h1_all, dy_all,
               dh1_ref, dw1_ref, dw2_ref, act, da, *scratch):
        comm.bind(None, h1_all, dy_all, mean_ref, rstd_ref, gain_ref, dh1_ref, scratch)
        i = pl.program_id(0)
        full, own = comm.full, comm.own

        def ticks(steps, k):
            for step in steps:
                todo = plans[step * 3 + k]
                if todo:
                    @pl.when(i == step)
                    def _():
                        for name, s in todo:
                            getattr(comm, name)(s)

        @pl.when(i == 0)
        def _():
            comm.begin()

        first = range(n_tiles)
        rest = range(n_tiles, grid)
        tidx = lax.div(i, 2) * 2 + lax.rem(i, 2) * comm.core + (1 - lax.rem(i, 2)) * (1 - comm.core)
        trow = pl.ds(pl.multiple_of(tidx * tile, tile), tile)
        pre_ref, dg_ref = comm.pre, comm.dg

        @pl.when(i < n_tiles)
        def _():
            z = (h1_tile[...].astype(F32) - comm.mu[trow, 0:1]) * comm.rs[trow, 0:1]
            n2 = (z * gain_ref[...]).astype(BF16)
            pre_ref[...] = dot(n2, w1[...])
        ticks(first, 0)

        @pl.when(i < n_tiles)
        def _():
            dg_ref[...] = dot(dy_tile[...], w2[...], 1, 1)
        ticks(first, 1)

        @pl.when(i < n_tiles)
        def _():
            pre = pre_ref[...]
            act[trow, :] = gelu_tanh(pre).astype(BF16)
            grad_pre = (dg_ref[...] * gelu_slope(pre)).astype(BF16)
            da[trow, :] = grad_pre
            part = dot(grad_pre, w1[...], 1, 1).astype(BF16)

            @pl.when(lax.rem(i, 2) == 0)
            def _():
                full[trow, :] = part

            @pl.when(lax.rem(i, 2) == 1)
            def _():
                own[lax.div(i, 2)] = part
        ticks(first, 2)

        @pl.when(i >= n_tiles)
        def _():
            c0 = pl.multiple_of((i - n_tiles) * cb, cb)
            z = (h1_col[...].astype(F32) - comm.mu[:, 0:1]) * comm.rs[:, 0:1]
            comm.n2c[...] = (z * gain_ref[:, pl.ds(c0, cb)]).astype(BF16)
        ticks(rest, 0)

        @pl.when(i >= n_tiles)
        def _():
            dw1_ref[...] = dot(comm.n2c[...], da[...], 0, 0).astype(BF16)
        ticks(rest, 1)

        @pl.when(i >= n_tiles)
        def _():
            dw2_ref[...] = dot(act[...], dy_col[...], 0, 0).astype(BF16)
        ticks(rest, 2)

        @pl.when(i == grid - 1)
        def _():
            comm.end()

    def wrapped(*refs):
        *most, pre, dg, n2c = refs
        comm.pre, comm.dg, comm.n2c = pre, dg, n2c
        kernel(*most)

    def tile_map(i):
        core = lax.rem(lax.axis_index('tp'), 2)
        ii = jnp.minimum(i, n_tiles - 1)
        odd = lax.rem(ii, 2)
        return lax.div(ii, 2) * 2 + odd * core + (1 - odd) * (1 - core), 0

    def col_at(i):
        return jnp.maximum(i - n_tiles, 0)

    whole = pl.BlockSpec(memory_space=VMEM)
    hbm = pl.BlockSpec(memory_space=ANY)
    return pl.pallas_call(
        wrapped,
        grid=(grid,),
        out_shape=(jax.ShapeDtypeStruct((rows, cols), BF16), jax.ShapeDtypeStruct((cols, ffn), BF16),
                   jax.ShapeDtypeStruct((ffn, cols), BF16)),
        in_specs=[pl.BlockSpec((tile, cols), tile_map), pl.BlockSpec((tile, cols), tile_map),
                  pl.BlockSpec((rows, cb), lambda i: (0, col_at(i))), pl.BlockSpec((rows, cb), lambda i: (0, col_at(i))),
                  whole, whole, whole, whole, whole, hbm, hbm],
        out_specs=(hbm, pl.BlockSpec((cb, ffn), lambda i: (col_at(i), 0)),
                   pl.BlockSpec((ffn, cb), lambda i: (0, col_at(i)))),
        scratch_shapes=[VMEM((rows, ffn), BF16), VMEM((rows, ffn), BF16)] + comm.scratch()
        + [VMEM((tile, ffn), F32), VMEM((tile, ffn), F32), VMEM((rows, cb), BF16)],
        compiler_params=pltpu.CompilerParams(collective_id=cid, has_side_effects=True, vmem_limit_bytes=VMEM_LIMIT,
                                             dimension_semantics=('arbitrary',)),
        name='mlp_stage',
    )(h1, dy, h1, dy, w_up, w_down, mean, rstd, gain, h1, dy)


def solution(mesh):
    act_spec = P('dp', None, None)
    stat_spec = P('dp', None)
    in_specs = (act_spec, act_spec, act_spec, stat_spec, stat_spec, stat_spec, stat_spec, P(), P(),
                P(None, 'tp', None, None), P('tp', None, None), P(None, 'tp'), P('tp', None))
    out_specs = (act_spec, P('dp', 'tp', None, None), P(('dp', 'tp'), None, None), P('dp', 'tp'),
                 P(('dp', 'tp'), None))
    n = mesh.shape['tp']

    def local_backward(x_saved, h1_saved, grad_y, mean_one, rstd_one, mean_two, rstd_two,
                       gain_one, gain_two, w_qkv, w_out, w_up, w_down):
        score_scale = w_qkv.shape[3] ** -0.5
        shape = x_saved.shape
        flat = (shape[0] * shape[1], shape[2])
        g1, g2 = gain_one.astype(F32)[None, :], gain_two.astype(F32)[None, :]
        dh1, grad_up, grad_down = mlp_stage(n, h1_saved.reshape(flat), grad_y.reshape(flat), mean_two, rstd_two, g2,
                                            w_up, w_down, 0)
        grad_h1 = dh1.reshape(shape)
        value_a8 = (x_saved.astype(F32) - mean_one[..., None]) * rstd_one[..., None]
        norm_one = (value_a8 * gain_one.astype(F32)).astype(BF16)
        qkv_acts = wide_einsum('msh,hncd->msncd', norm_one, w_qkv).astype(BF16)
        grad_o = wide_einsum('msh,ndh->msnd', grad_h1, w_out).astype(BF16)
        attn_out, grad_qkv = attention_backward(qkv_acts[:, :, :, 0], qkv_acts[:, :, :, 1], qkv_acts[:, :, :, 2],
                                                grad_o, score_scale)
        grad_out_w = wide_einsum('msnd,msh->ndh', attn_out, grad_h1).astype(BF16)
        grad_qkv_w = wide_einsum('msh,msncd->hncd', norm_one, grad_qkv).astype(BF16)
        part_one = wide_einsum('msncd,hncd->msh', grad_qkv, w_qkv).astype(BF16)
        dx = reduce_norm_gather(n, part_one.reshape(flat), x_saved.reshape(flat), dh1, mean_one, rstd_one, g1, 1)
        return dx.reshape(shape), grad_qkv_w, grad_out_w, grad_up, grad_down

    return jax.shard_map(local_backward, mesh=mesh, in_specs=in_specs, out_specs=out_specs, check_vma=False)
```

profile of v0, /device:TPU:97, one launch (start us, length us, event | category | flops | bytes accessed | tf_op | source)
XLA Modules:
  0.0 287.4 jit_solution(7419676536462890496)
XLA Ops:
  0.6 0.7 convert_element_type.81
  1.3 0.0 copy-start.4
  1.3 1.3 broadcast_in_dim.29
  2.6 0.3 iota_compare_fusion
  2.9 0.0 copy-done.4
  2.9 7.9 %fusion.41 = bf16[2,1024,1,3,96]{1,4,3,0,2:T(8,128)(2,1)S(1)} fusion(bf16[3072,1,3,96]{0,3,2,1:T(8,128)(2,1)} %param.22, f32[3072]{0:T(1024)S(1)} %convert_element_type.81, f32[2,1024]{1,0:T(2,128)} %rstd_ref.1, f32[2,1024]{1,0:T(2,128)} %mean_ref.1, bf16[2,1024,3072]{2,1,0:T(8,128)(2,1)} %param.13), kind=kOutput, calls=%fused_computation.34 | convolution fusion | flops 3655925760 | bytes 15560704 | tf_op jit(solution)/shard_map/msh,hncd->msncd/dot_general | solution.py:570
  10.9 0.0 copy-start.2
  10.9 6.0 %fusion.85 = (f32[2,1024]{1,0:T(2,128)}, f32[2,1024,1024]{1,2,0:T(8,128)}) fusion(pred[1024,1024]{0,1:T(8,128)(4,1)S(1)} %iota_compare_fusion, bf16[2,1024,1,3,96]{1,4,3,0,2:T(8,128)(2,1)S(1)} %fusion.41), kind=kOutput, calls=%fused_computation.60 | convolution fusion | flops 411042816 | bytes 10231808 | tf_op jit(solution)/shard_map/sub | solution.py:35
  16.9 0.0 copy-done.2
  16.9 102.1 %mlp_stage.1 = (bf16[2048,3072]{1,0:T(8,128)(2,1)}, bf16[3072,384]{1,0:T(8,128)(2,1)}, bf16[384,3072]{1,0:T(8,128)(2,1)}) custom-call(bf16[2048,3072]{1,0:T(8,128)(2,1)} %bitcast.125, bf16[2048,3072]{1,0:T(8,128)(2,1)} %bitcast.128, bf16[2048,3072]{1,0:T(8,128)(2,1)} %bitcast.126, bf16[2048,3072]{1,0:T(8,128)(2,1)} %bitcast.129, bf16[3072,384]{1,0:T(8,128)(2,1)} %refs_4_.1, ...), custom_call_target="tpu_custom_call" | custom-call | tf_op jit(solution)/shard_map/mlp_stage/pallas_call | solution.py:532
  119.0 0.0 copy-start.9
  119.0 0.0 copy-start.10
  119.0 8.8 %convolution_convert_fusion = bf16[2,1024,96]{1,2,0:T(8,128)(2,1)S(1)} fusion(bf16[2,1024,3072]{2,1,0:T(8,128)(2,1)} %bitcast.133, bf16[1,96,3072]{2,1,0:T(8,128)(2,1)} %param.23), kind=kOutput, calls=%fused_computation.39 | convolution fusion | flops 1208156160 | bytes 13565952 | tf_op jit(solution)/shard_map/msh,ndh->msnd/dot_general | solution.py:571
  127.8 0.0 copy-done.9
  127.8 0.0 copy-done.10
  127.8 0.0 copy-start.3
  127.9 1.4 fusion.67
  129.3 0.0 copy-done.3
  129.3 10.6 %fusion.29 = bf16[1,96,3072]{2,1,0:T(8,128)(2,1)} fusion(bf16[2,1024,3072]{2,1,0:T(8,128)(2,1)} %bitcast.134, bf16[2,1024,1,3,96]{1,4,3,0,2:T(8,128)(2,1)S(1)} %copy-done.3, f32[2,1024,1024]{1,2,0:T(8,128)} %get-tuple-element.12, f32[2,1024]{1,0:T(2,128)S(1)} %copy-done.10), kind=kOutput, calls=%fused_computation.26 | convolution fusion | flops 1615298560 | bytes 21962752 | tf_op jit(solution)/shard_map/msnd,msh->ndh/dot_general | solution.py:574
  139.9 4.5 %fusion.75 = f32[2,1024,1024]{1,2,0:T(8,128)} fusion(bf16[2,1024,96]{1,2,0:T(8,128)(2,1)S(1)} %convolution_convert_fusion, bf16[2,1024,1,3,96]{1,4,3,0,2:T(8,128)(2,1)S(1)} %copy-done.3), kind=kOutput, calls=%fused_computation.50 | convolution fusion | flops 402653184 | bytes 9175040 | tf_op jit(solution)/shard_map/bqnd,bknd->bnqk/dot_general | solution.py:39
  144.4 14.0 %fusion.61 = bf16[2,1024,1,1,96]{1,4,0,3,2:T(8,128)(2,1)S(1)} fusion(f32[2,1024,1024]{1,2,0:T(8,128)} %fusion.75, bf16[2,1024,1,3,96]{1,4,3,0,2:T(8,128)(2,1)S(1)} %copy-done.3, f32[2,1024,1024]{1,2,0:T(8,128)} %get-tuple-element.12, f32[2,1024]{1,0:T(2,128)S(1)} %copy-done.10), kind=kOutput, calls=%fused_computation.41 | convolution fusion | flops 417532928 | bytes 34357248 | tf_op jit(solution)/shard_map/bnqk,bknd->bqnd/dot_general | solution.py:42
  158.4 0.0 copy-start.5
  158.5 0.0 copy-start.6
  158.5 0.0 copy-start.7
  158.5 13.0 %fusion.58 = bf16[2,1024,1,1,96]{1,4,0,3,2:T(8,128)(2,1)S(1)} fusion(f32[2,1024,1024]{1,2,0:T(8,128)} %fusion.75, bf16[2,1024,1,3,96]{1,4,3,0,2:T(8,128)(2,1)S(1)} %copy-done.3, f32[2,1024,1024]{1,2,0:T(8,128)} %get-tuple-element.12, f32[2,1024]{1,0:T(2,128)S(1)} %copy-done.10), kind=kOutput, calls=%fused_computation.40 | convolution fusion | flops 417532928 | bytes 34357248 | tf_op jit(solution)/shard_map/bnqk,bqnd->bknd/dot_general | solution.py:43
  171.4 0.0 copy-done.5
  171.5 0.0 copy-done.6
  171.5 0.0 copy-done.7
  171.5 0.0 copy-start.8
  171.5 10.8 %fusion.25 = bf16[3072,1,3,96]{0,3,2,1:T(8,128)(2,1)} fusion(f32[3072]{0:T(1024)S(1)} %copy-done.5, f32[2,1024]{1,0:T(2,128)S(1)} %copy-done.6, f32[2,1024]{1,0:T(2,128)S(1)} %copy-done.7, bf16[2,1024,3072]{2,1,0:T(8,128)(2,1)} %param.13, bf16[2,1024,1,1,96]{1,4,0,3,2:T(8,128)(2,1)S(1)} %fusion.67, bf16[2,1024,1,1,96]{1,4,0,3,2:T(8,128)(2,1)S(1)} %fusion.58, ...), kind=kOutput, calls=%fused_computation.23 | convolution fusion | flops 3659759616 | bytes 15560704 | tf_op jit(solution)/shard_map/msh,msncd->hncd/dot_general | solution.py:575
  182.3 0.0 copy-done.8
  182.3 9.7 %bitcast_convert_fusion = bf16[2,1024,3072]{2,1,0:T(8,128)(2,1)} fusion(bf16[3072,1,3,96]{0,3,2,1:T(8,128)(2,1)S(1)} %copy-done.8, bf16[2,1024,1,1,96]{1,4,0,3,2:T(8,128)(2,1)S(1)} %fusion.67, bf16[2,1024,1,1,96]{1,4,0,3,2:T(8,128)(2,1)S(1)} %fusion.58, bf16[2,1024,1,1,96]{1,4,0,3,2:T(8,128)(2,1)S(1)} %fusion.61), kind=kOutput, calls=%fused_computation.2 | convolution fusion | flops 3631349760 | bytes 15532032 | tf_op jit(solution)/shard_map/msncd,hncd->msh/dot_general | solution.py:576
  192.0 80.9 %sum_norm_gather_1.1 = bf16[2048,3072]{1,0:T(8,128)(2,1)} custom-call(bf16[2048,3072]{1,0:T(8,128)(2,1)} %bitcast.135, bf16[2048,3072]{1,0:T(8,128)(2,1)} %bitcast.132, bf16[2048,3072]{1,0:T(8,128)(2,1)} %get-tuple-element.8.resid_ref, f32[2,1024]{1,0:T(2,128)} %mean_ref.1, f32[2,1024]{1,0:T(2,128)} %rstd_ref.1, f32[1,3072]{1,0:T(1,128)} %bitcast.136), custom_call_target="tpu_custom_call" | custom-call | tf_op jit(solution)/shard_map/sum_norm_gather_1/pallas_call | solution.py:410
  272.9 0.0 copy-start.1
  272.9 0.0 copy-start
  272.9 11.4 %copy.34 = bf16[2,1024,3072]{2,1,0:T(8,128)(2,1)} copy(bf16[2,1024,3072]{2,1,0:T(8,128)(2,1)} %bitcast.131) | data formatting | bytes 25165824
  284.4 0.0 copy-done.1
  284.4 1.4 copy.35
  285.8 0.0 copy-done
  285.8 1.4 copy.36
Async XLA Ops:
  1.3 1.6 copy-start.4
  10.9 6.0 %copy-start.2 = (bf16[2,1024,1,3,96]{1,4,3,0,2:T(8,128)(2,1)}, bf16[2,1024,1,3,96]{1,4,3,0,2:T(8,128)(2,1)S(1)}, u32[]{:S(2)}) copy-start(bf16[2,1024,1,3,96]{1,4,3,0,2:T(8,128)(2,1)S(1)} %fusion.41) | copy-start | bytes 3538948
  119.0 8.8 %copy-start.9 = (f32[2,1024,1024]{1,2,0:T(8,128)S(1)}, f32[2,1024,1024]{1,2,0:T(8,128)}, u32[]{:S(2)}) copy-start(f32[2,1024,1024]{1,2,0:T(8,128)} %get-tuple-element.12) | copy-start | bytes 25165828
  119.0 8.8 %copy-start.10 = (f32[2,1024]{1,0:T(2,128)S(1)}, f32[2,1024]{1,0:T(2,128)}, u32[]{:S(2)}) copy-start(f32[2,1024]{1,0:T(2,128)} %get-tuple-element.11) | copy-start | bytes 24580
  127.8 1.4 copy-start.3
  158.4 13.0 %copy-start.5 = (f32[3072]{0:T(1024)S(1)}, f32[3072]{0:T(1024)}, u32[]{:S(2)}) copy-start(f32[3072]{0:T(1024)} %copy-done.4) | copy-start | bytes 36868
  158.5 13.0 %copy-start.6 = (f32[2,1024]{1,0:T(2,128)S(1)}, f32[2,1024]{1,0:T(2,128)}, u32[]{:S(2)}) copy-start(f32[2,1024]{1,0:T(2,128)} %rstd_ref.1) | copy-start | bytes 24580
  158.5 13.0 %copy-start.7 = (f32[2,1024]{1,0:T(2,128)S(1)}, f32[2,1024]{1,0:T(2,128)}, u32[]{:S(2)}) copy-start(f32[2,1024]{1,0:T(2,128)} %mean_ref.1) | copy-start | bytes 24580
  171.5 10.8 %copy-start.8 = (bf16[3072,1,3,96]{0,3,2,1:T(8,128)(2,1)S(1)}, bf16[3072,1,3,96]{0,3,2,1:T(8,128)(2,1)}, u32[]{:S(2)}) copy-start(bf16[3072,1,3,96]{0,3,2,1:T(8,128)(2,1)} %param.22) | copy-start | bytes 5308420
  272.9 11.5 %copy-start.1 = (bf16[3072,384]{1,0:T(8,128)(2,1)S(1)}, bf16[3072,384]{1,0:T(8,128)(2,1)}, u32[]{:S(2)}) copy-start(bf16[3072,384]{1,0:T(8,128)(2,1)} %get-tuple-element.21) | copy-start | bytes 7077892
  272.9 12.9 %copy-start = (bf16[384,3072]{1,0:T(8,128)(2,1)S(1)}, bf16[384,3072]{1,0:T(8,128)(2,1)}, u32[]{:S(2)}) copy-start(bf16[384,3072]{1,0:T(8,128)(2,1)} %get-tuple-element.22) | copy-start | bytes 7077892
where the time goes:
time: 291 us; the launch traced here: 287 us
  Pallas kernels  183 us (63%)
  matrix products  86.7 us (30%)
  local copies, waits for them, and re-layouts  14.3 us (5%)
    pallas_call x1, Pallas kernels, mlp_stage(): pl.pallas_call(wrapped, grid=(grid,), out_shape=(jax.ShapeDtypeStruct((ro...  102 us
    pallas_call x1, Pallas kernels, reduce_norm_gather(): pl.pallas_call(kernel, out_shape=jax.ShapeDtypeStruct((rows, cols), BF16)...  80.9 us
    unnamed x25, local copies, waits for them, and re-layouts  14.3 us
    dot_general x1, matrix products, attention_backward(): grad_q = wide_einsum('bnqk,bknd->bqnd', grad_s, k_heads).astype(BF16)  14 us
    dot_general x1, matrix products, attention_backward(): grad_k = wide_einsum('bnqk,bqnd->bknd', grad_s, q_heads).astype(BF16)  13 us
    dot_general x1, matrix products, local_backward(): grad_qkv_w = wide_einsum('msh,msncd->hncd', norm_one, grad_qkv).astype(BF16)  10.8 us
    dot_general x1, matrix products, local_backward(): grad_out_w = wide_einsum('msnd,msh->ndh', attn_out, grad_h1).astype(BF16)  10.6 us
    dot_general x1, matrix products, local_backward(): part_one = wide_einsum('msncd,hncd->msh', grad_qkv, w_qkv).astype(BF16)  9.7 us

commit v1 on v0

--- a/solution.py
+++ b/solution.py
@@ -5,7 +5,6 @@
 from jax.experimental import pallas as pl
 from jax.experimental.pallas import tpu as pltpu
 from jax.sharding import PartitionSpec as P
-from functools import partial
 
 GELU_C = 0.7978845608028654
 GELU_A = 0.044715
@@ -13,7 +12,6 @@
 BF16 = jnp.bfloat16
 ANY = pl.ANY
 VMEM = pltpu.VMEM
-wide_einsum = partial(jnp.einsum, preferred_element_type=F32)
 
 
 def gelu_tanh(pre_act):
@@ -26,22 +24,6 @@
     tanh_val = jnp.tanh(inner_arg)
     return (0.5 * (1.0 + tanh_val)
             + 0.5 * pre_act * (1.0 - tanh_val * tanh_val) * GELU_C * (1.0 + 3.0 * GELU_A * pre_act * pre_act))
-
-
-def attention_backward(q_heads, k_heads, v_heads, grad_o, score_scale):
-    seq_len = q_heads.shape[1]
-    scores = wide_einsum('bqnd,bknd->bnqk', q_heads, k_heads) * score_scale
-    causal = jnp.arange(seq_len)[:, None] >= jnp.arange(seq_len)[None, :]
-    attn_prob = jax.nn.softmax(jnp.where(causal, scores, -1e30), axis=-1)
-    prob_bf16 = attn_prob.astype(BF16)
-    attn_out = wide_einsum('bnqk,bknd->bqnd', prob_bf16, v_heads).astype(BF16)
-    grad_v = wide_einsum('bnqk,bqnd->bknd', prob_bf16, grad_o).astype(BF16)
-    grad_p = wide_einsum('bqnd,bknd->bnqk', grad_o, v_heads)
-    row_dot = jnp.sum(attn_prob * grad_p, axis=-1, keepdims=True)
-    grad_s = (attn_prob * (grad_p - row_dot) * score_scale).astype(BF16)
-    grad_q = wide_einsum('bnqk,bknd->bqnd', grad_s, k_heads).astype(BF16)
-    grad_k = wide_einsum('bnqk,bqnd->bknd', grad_s, q_heads).astype(BF16)
-    return attn_out, jnp.stack([grad_q, grad_k, grad_v], axis=3)
 
 
 BLOCK = 512
@@ -394,30 +376,6 @@
 VMEM_LIMIT = 64 * 1024 * 1024 - 64 * 1024
 
 
-def reduce_norm_gather(n, part, saved, resid, mean, rstd, gain, cid):
-    rows, cols = part.shape
-    comm = Comm(n, rows, cols)
-    comm.part_given = True
-    plans = comm.plan([(3.0, [(s, w) for s in range(comm.streams) for w in ('pair', 'own')])])
-
-    def kernel(part_ref, saved_ref, resid_ref, mean_ref, rstd_ref, gain_ref, out_ref, *scratch):
-        comm.bind(part_ref, saved_ref, resid_ref, mean_ref, rstd_ref, gain_ref, out_ref, scratch)
-        comm.begin()
-        for name, s in plans[0]:
-            getattr(comm, name)(s)
-        comm.end()
-
-    return pl.pallas_call(
-        kernel,
-        out_shape=jax.ShapeDtypeStruct((rows, cols), BF16),
-        in_specs=[pl.BlockSpec(memory_space=ANY)] * 3 + [pl.BlockSpec(memory_space=VMEM)] * 3,
-        out_specs=pl.BlockSpec(memory_space=ANY),
-        scratch_shapes=comm.scratch(),
-        compiler_params=pltpu.CompilerParams(collective_id=cid, has_side_effects=True, vmem_limit_bytes=VMEM_LIMIT),
-        name='sum_norm_gather_%d' % cid,
-    )(part, saved, resid, mean, rstd, gain)
-
-
 def dot(a, b, ca=1, cb=0):
     return lax.dot_general(a, b, (((ca,), (cb,)), ((), ())), preferred_element_type=F32)
 
@@ -547,6 +505,195 @@
     )(h1, dy, h1, dy, w_up, w_down, mean, rstd, gain, h1, dy)
 
 
+def attention_stage(n, mbs, x, dh1, mean, rstd, gain, w_qkv, w_out, score_scale, cid):
+    rows, cols = x.shape
+    seq = rows // mbs
+    hd = w_out.shape[0]
+    qkv_w = w_qkv.shape[1]
+    comm = Comm(n, rows, cols)
+    tile = comm.half
+    per_mb = seq // tile
+    n_seq = 2 * per_mb * mbs
+    cb = 256
+    n_cols = cols // cb
+    grid = n_seq + n_cols
+    points = []
+    for b in range(mbs):
+        points += [(1.4, []), (0.4, []), (0.4, [])] * per_mb
+        for j in range(per_mb - 1, -1, -1):
+            s = b * (per_mb // 2) + j // 2
+            points += [(1.4, []), (1.4, []), (1.2, [(s, 'pair'), (s, 'own')] if j % 2 == 0 else [])]
+    for i in range(n_cols):
+        points += [(0.7, []), (0.8, []), (0.6, [])]
+    plans = comm.plan(points)
+
+    def kernel(x_tile, dh_tile, x_col, dh_col, wqkv, wo, mean_ref, rstd_ref, gain_ref, x_all, dh_all,
+               dx_ref, dwqkv_ref, dwo_ref, qkv, do, o_all, dqkv, dk_acc, dv_acc, n1c, p_ref, *scratch):
+        comm.bind(None, x_all, dh_all, mean_ref, rstd_ref, gain_ref, dx_ref, scratch)
+        i = pl.program_id(0)
+        full, own = comm.full, comm.own
+
+        def ticks(steps, k):
+            for step in steps:
+                todo = plans[step * 3 + k]
+                if todo:
+                    @pl.when(i == step)
+                    def _():
+                        for name, s in todo:
+                            getattr(comm, name)(s)
+
+        @pl.when(i == 0)
+        def _():
+            comm.begin()
+
+        span = 2 * per_mb
+        first = range(n_seq)
+        rest = range(n_seq, grid)
+        b = lax.div(i, span)
+        at = lax.rem(i, span)
+        in_seq = i < n_seq
+        loading = jnp.logical_and(in_seq, at < per_mb)
+        base = b * seq
+        trow = pl.ds(pl.multiple_of(jnp.minimum(base + at * tile, rows - tile), tile), tile)
+
+        @pl.when(loading)
+        def _():
+            z = (x_tile[...].astype(F32) - comm.mu[trow, 0:1]) * comm.rs[trow, 0:1]
+            n1 = (z * gain_ref[...]).astype(BF16)
+            qkv[trow, :] = dot(n1, wqkv[...]).astype(BF16)
+
+        def variants(fn):
+            for j in range(per_mb):
+                @pl.when(jnp.logical_and(in_seq, at == 2 * per_mb - 1 - j))
+                def _():
+                    fn(j)
+
+        def part_a(j):
+            size = (j + 1) * tile
+            mine = pl.ds(pl.multiple_of(base + j * tile, tile), tile)
+            keys = pl.ds(pl.multiple_of(base, tile), size)
+            s = dot(qkv[mine, 0:hd], qkv[keys, hd:2 * hd], 1, 1) * score_scale
+            row = lax.broadcasted_iota(jnp.int32, (tile, size), 0) + j * tile
+            col = lax.broadcasted_iota(jnp.int32, (tile, size), 1)
+            s = jnp.where(row >= col, s, -1e30)
+            e = jnp.exp(s - jnp.max(s, axis=-1, keepdims=True))
+            p = e / jnp.sum(e, axis=-1, keepdims=True)
+            p_ref[:, 0:size] = p
+            pb = p.astype(BF16)
+            o_all[mine, :] = dot(pb, qkv[keys, 2 * hd:3 * hd]).astype(BF16)
+            dv = dot(pb, do[mine, :], 0, 0)
+            if j == per_mb - 1:
+                dv_acc[...] = dv
+            else:
+                dv_acc[0:size, :] += dv
+
+        def part_b(j):
+            size = (j + 1) * tile
+            mine = pl.ds(pl.multiple_of(base + j * tile, tile), tile)
+            keys = pl.ds(pl.multiple_of(base, tile), size)
+            p = p_ref[:, 0:size]
+            dp = dot(do[mine, :], qkv[keys, 2 * hd:3 * hd], 1, 1)
+            rd = jnp.sum(p * dp, axis=-1, keepdims=True)
+            ds = (p * (dp - rd) * score_scale).astype(BF16)
+            dqkv[mine, 0:hd] = dot(ds, qkv[keys, hd:2 * hd]).astype(BF16)
+            dk = dot(ds, qkv[mine, 0:hd], 0, 0)
+            if j == per_mb - 1:
+                dk_acc[...] = dk
+            else:
+                dk_acc[0:size, :] += dk
+            dqkv[mine, hd:2 * hd] = dk_acc[j * tile:size, :].astype(BF16)
+            dqkv[mine, 2 * hd:3 * hd] = dv_acc[j * tile:size, :].astype(BF16)
+
+        def part_c(j):
+            mine = pl.ds(pl.multiple_of(base + j * tile, tile), tile)
+            part = dot(dqkv[mine, :], wqkv[...], 1, 1).astype(BF16)
+
+            @pl.when(comm.core == j % 2)
+            def _():
+                own[b * (per_mb // 2) + j // 2] = part
+
+            @pl.when(comm.core != j % 2)
+            def _():
+                full[mine, :] = part
+
+        variants(part_a)
+        ticks(first, 0)
+
+        @pl.when(loading)
+        def _():
+            do[trow, :] = dot(dh_tile[...], wo[...], 1, 1).astype(BF16)
+
+        variants(part_b)
+        ticks(first, 1)
+        variants(part_c)
+        ticks(first, 2)
+
+        @pl.when(i >= n_seq)
+        def _():
+            c0 = pl.multiple_of((i - n_seq) * cb, cb)
+            z = (x_col[...].astype(F32) - comm.mu[:, 0:1]) * comm.rs[:, 0:1]
+            n1c[...] = (z * gain_ref[:, pl.ds(c0, cb)]).astype(BF16)
+        ticks(rest, 0)
+
+        @pl.when(i >= n_seq)
+        def _():
+            dwqkv_ref[...] = dot(n1c[...], dqkv[...], 0, 0).astype(BF16)
+        ticks(rest, 1)
+
+        @pl.when(i >= n_seq)
+        def _():
+            dwo_ref[...] = dot(o_all[...], dh_col[...], 0, 0).astype(BF16)
+        ticks(rest, 2)
+
+        @pl.when(i == grid - 1)
+        def _():
+            comm.end()
+
+    def tile_map(i):
+        ii = jnp.minimum(i, n_seq - 1)
+        return lax.div(ii, 2 * per_mb) * per_mb + jnp.minimum(lax.rem(ii, 2 * per_mb), per_mb - 1), 0
+
+    def col_at(i):
+        return jnp.maximum(i - n_seq, 0)
+
+    whole = pl.BlockSpec(memory_space=VMEM)
+    hbm = pl.BlockSpec(memory_space=ANY)
+    return pl.pallas_call(
+        kernel,
+        grid=(grid,),
+        out_shape=(jax.ShapeDtypeStruct((rows, cols), BF16), jax.ShapeDtypeStruct((cols, qkv_w), BF16),
+                   jax.ShapeDtypeStruct((hd, cols), BF16)),
+        in_specs=[pl.BlockSpec((tile, cols), tile_map), pl.BlockSpec((tile, cols), tile_map),
+                  pl.BlockSpec((rows, cb), lambda i: (0, col_at(i))), pl.BlockSpec((rows, cb), lambda i: (0, col_at(i))),
+                  whole, whole, whole, whole, whole, hbm, hbm],
+        out_specs=(hbm, pl.BlockSpec((cb, qkv_w), lambda i: (col_at(i), 0)),
+                   pl.BlockSpec((hd, cb), lambda i: (0, col_at(i)))),
+        scratch_shapes=[VMEM((rows, qkv_w), BF16), VMEM((rows, hd), BF16), VMEM((rows, hd), BF16),
+                        VMEM((rows, qkv_w), BF16), VMEM((seq, hd), F32), VMEM((seq, hd), F32), VMEM((rows, cb), BF16),
+                        VMEM((tile, seq), F32)] + comm.scratch(),
+        compiler_params=pltpu.CompilerParams(collective_id=cid, has_side_effects=True, vmem_limit_bytes=VMEM_LIMIT,
+                                             dimension_semantics=('arbitrary',)),
+        name='attention_stage',
+    )(x, dh1, x, dh1, w_qkv, w_out, mean, rstd, gain, x, dh1)
+
+
+def spread_copy(arr):
+    rows, cols = arr.shape
+    tile = 256
+
+    def kernel(src, dst):
+        dst[...] = src[...]
+
+    return pl.pallas_call(
+        kernel,
+        grid=(rows // tile,),
+        out_shape=jax.ShapeDtypeStruct(arr.shape, arr.dtype),
+        in_specs=[pl.BlockSpec((tile, cols), lambda i: (i, 0))],
+        out_specs=pl.BlockSpec((tile, cols), lambda i: (i, 0)),
+        name='spread_copy',
+    )(arr)
+
+
 def solution(mesh):
     act_spec = P('dp', None, None)
     stat_spec = P('dp', None)
@@ -564,17 +711,14 @@
         g1, g2 = gain_one.astype(F32)[None, :], gain_two.astype(F32)[None, :]
         dh1, grad_up, grad_down = mlp_stage(n, h1_saved.reshape(flat), grad_y.reshape(flat), mean_two, rstd_two, g2,
                                             w_up, w_down, 0)
-        grad_h1 = dh1.reshape(shape)
-        value_a8 = (x_saved.astype(F32) - mean_one[..., None]) * rstd_one[..., None]
-        norm_one = (value_a8 * gain_one.astype(F32)).astype(BF16)
-        qkv_acts = wide_einsum('msh,hncd->msncd', norm_one, w_qkv).astype(BF16)
-        grad_o = wide_einsum('msh,ndh->msnd', grad_h1, w_out).astype(BF16)
-        attn_out, grad_qkv = attention_backward(qkv_acts[:, :, :, 0], qkv_acts[:, :, :, 1], qkv_acts[:, :, :, 2],
-                                                grad_o, score_scale)
-        grad_out_w = wide_einsum('msnd,msh->ndh', attn_out, grad_h1).astype(BF16)
-        grad_qkv_w = wide_einsum('msh,msncd->hncd', norm_one, grad_qkv).astype(BF16)
-        part_one = wide_einsum('msncd,hncd->msh', grad_qkv, w_qkv).astype(BF16)
-        dx = reduce_norm_gather(n, part_one.reshape(flat), x_saved.reshape(flat), dh1, mean_one, rstd_one, g1, 1)
-        return dx.reshape(shape), grad_qkv_w, grad_out_w, grad_up, grad_down
+        heads, _, width = w_qkv.shape[1:]
+        pad = -width % 128
+        wide_qkv = jnp.pad(w_qkv[:, 0], ((0, 0), (0, 0), (0, pad))).reshape(flat[1], -1)
+        wide_out = jnp.pad(w_out[0], ((0, pad), (0, 0)))
+        dx, dqkv_w, dout_w = attention_stage(n, shape[0], x_saved.reshape(flat), dh1, mean_one, rstd_one, g1,
+                                             wide_qkv, wide_out, score_scale, 1)
+        grad_qkv_w = dqkv_w.reshape(flat[1], heads, 3, width + pad)[..., :width]
+        grad_out_w = dout_w[None, :width]
+        return spread_copy(dx).reshape(shape), grad_qkv_w, grad_out_w, grad_up, grad_down
 
     return jax.shard_map(local_backward, mesh=mesh, in_specs=in_specs, out_specs=out_specs, check_vma=False)

time: 291 us -> 252 us (0.87)
  matrix products: 86.7 us -> 0 us
  Pallas kernels: 183 us -> 232 us
    dot_general x9 -> x0, matrix products: 80.7 us -> none  [the longest x1 14 us: attention_backward(): grad_q = wide_einsum('bnqk,bknd->bqnd', grad_s, k_heads).astype(BF16)]
    pallas_call x1 -> x2, Pallas kernels: 80.9 us -> 130 us  [the longest x1 119 us: attention_stage(): pl.pallas_call(kernel, grid=(grid,), out_shape=(jax.ShapeDtypeStruct((row...]
    unnamed x25 -> x8, local copies, waits for them, and re-layouts: 14.3 us -> 4.9 us
    sub x1 -> x0, matrix products: 5.97 us -> none  [attention_backward(): attn_prob = jax.nn.softmax(jnp.where(causal, scores, -1e+30), axis=-1)]
    pad x0 -> x2, local copies, waits for them, and re-layouts: none -> 3.73 us  [the longest x1 2.01 us: local_backward(): wide_out = jnp.pad(w_out[0], ((0, pad), (0, 0)))]
where the time goes in v1:
time: 252 us; the launch traced here: 251 us
  Pallas kernels  232 us (92%)
  local copies, waits for them, and re-layouts  16.1 us (6%)
  other arithmetic  2.59 us (1%)
    pallas_call x1, Pallas kernels, attention_stage(): pl.pallas_call(kernel, grid=(grid,), out_shape=(jax.ShapeDtypeStruct((row...  119 us
    pallas_call x1, Pallas kernels, mlp_stage(): pl.pallas_call(wrapped, grid=(grid,), out_shape=(jax.ShapeDtypeStruct((ro...  101 us
    pallas_call x1, Pallas kernels, spread_copy(): pl.pallas_call(kernel, grid=(rows // tile,), out_shape=jax.ShapeDtypeStru...  11.4 us

profile of v1, /device:TPU:97, one launch (start us, length us, event | category | flops | bytes accessed | tf_op | source)
XLA Modules:
  0.0 251.0 jit_solution(5554150583859457498)
XLA Ops:
  0.6 1.3 broadcast_in_dim.19
  1.9 1.3 broadcast_in_dim.18
  3.2 2.0 pad.9.wo
  5.2 1.7 pad.8
  7.0 2.4 copy.20.wqkv
  9.4 101.3 %mlp_stage.1 = (bf16[2048,3072]{1,0:T(8,128)(2,1)}, bf16[3072,384]{1,0:T(8,128)(2,1)}, bf16[384,3072]{1,0:T(8,128)(2,1)}) custom-call(bf16[2048,3072]{1,0:T(8,128)(2,1)} %bitcast.12, bf16[2048,3072]{1,0:T(8,128)(2,1)} %bitcast.15, bf16[2048,3072]{1,0:T(8,128)(2,1)} %bitcast.13, bf16[2048,3072]{1,0:T(8,128)(2,1)} %bitcast.16, bf16[3072,384]{1,0:T(8,128)(2,1)} %refs_4_.1, ...), custom_call_target="tpu_custom_call" | custom-call | tf_op jit(solution)/shard_map/mlp_stage/pallas_call | solution.py:490
  110.7 119.0 %attention_stage.1 = (bf16[2048,3072]{1,0:T(8,128)(2,1)}, bf16[3072,384]{1,0:T(8,128)(2,1)}, bf16[128,3072]{1,0:T(8,128)(2,1)}) custom-call(bf16[2048,3072]{1,0:T(8,128)(2,1)} %bitcast.18, bf16[2048,3072]{1,0:T(8,128)(2,1)} %get-tuple-element.11.dh_tile.dh_col.dh_all, bf16[2048,3072]{1,0:T(8,128)(2,1)} %bitcast.19, ...), custom_call_target="tpu_custom_call" | custom-call | tf_op jit(solution)/shard_map/attention_stage/pallas_call | solution.py:661
  229.6 0.0 copy-start.2
  229.6 11.4 %spread_copy.1 = bf16[2048,3072]{1,0:T(8,128)(2,1)} custom-call(bf16[2048,3072]{1,0:T(8,128)(2,1)} %get-tuple-element.12.src), custom_call_target="tpu_custom_call" | custom-call | tf_op jit(solution)/shard_map/spread_copy/pallas_call | solution.py:687
  241.1 0.0 copy-done.2
  241.1 0.9 slice_bitcast_fusion
  241.9 2.8 %copy.21 = bf16[3072,384]{0,1:T(8,128)(2,1)S(1)} copy(bf16[3072,384]{1,0:T(8,128)(2,1)} %get-tuple-element.13) | data formatting | bytes 4718592 | tf_op jit(solution)/shard_map/attention_stage/pallas_call | solution.py:661
  244.8 0.0 copy-start.1
  244.8 1.3 slice.8
  246.1 1.0 copy-done.1
  247.1 0.0 copy-start
  247.1 1.4 copy.24
  248.5 1.1 copy-done
  249.6 1.4 copy.25
Async XLA Ops:
  229.6 11.5 %copy-start.2 = (bf16[128,3072]{1,0:T(8,128)(2,1)S(1)}, bf16[128,3072]{1,0:T(8,128)(2,1)}, u32[]{:S(2)}) copy-start(bf16[128,3072]{1,0:T(8,128)(2,1)} %get-tuple-element.14) | copy-start | bytes 2359300
  244.8 2.3 copy-start.1
  247.1 2.5 %copy-start = (bf16[384,3072]{1,0:T(8,128)(2,1)S(1)}, bf16[384,3072]{1,0:T(8,128)(2,1)}, u32[]{:S(2)}) copy-start(bf16[384,3072]{1,0:T(8,128)(2,1)} %get-tuple-element.26) | copy-start | bytes 7077892

commit v2 on v1

--- a/solution.py
+++ b/solution.py
@@ -28,8 +28,8 @@
 
 BLOCK = 512
 SEMS = 32
-LINK = {'1+': 85e3, '1-': 85e3, '2+': 85e3, '2-': 85e3, 'D': 450e3}
-LATENCY = 2.3
+LINK = {'+': 90e3, '-': 90e3, 'D': 450e3}
+LATENCY = 2.6
 TICK = 0.3
 
 
@@ -59,6 +59,7 @@
             VMEM((ns, l2, w), BF16),
             VMEM((self.rows, 128), F32),
             VMEM((self.rows, 128), F32),
+            VMEM((1, w), F32),
             pltpu.SemaphoreType.DMA((ns, SEMS)),
             pltpu.SemaphoreType.DMA((ns, SEMS)),
             pltpu.SemaphoreType.DMA((ns, 8)),
@@ -66,9 +67,9 @@
         ]
 
     def bind(self, part, saved, resid, mean, rstd, gain, out, scratch):
-        (self.own, self.pair, self.ring1, self.ring2, self.full, self.zrow, self.rrow, self.mu, self.rs,
+        (self.own, self.pair, self.ring1, self.ring2, self.full, self.zrow, self.rrow, self.mu, self.rs, self.gain,
          self.ssem, self.rsem, self.lsem, self.freed) = scratch
-        self.part, self.saved, self.resid, self.gain, self.out = part, saved, resid, gain, out
+        self.part, self.saved, self.resid, self.gain_in, self.out = part, saved, resid, gain, out
         self.mean, self.rstd = mean, rstd
         side = self.side
         me = lax.axis_index('tp')
@@ -183,6 +184,7 @@
         pl.semaphore_wait(sem, len(peers))
 
     def columns(self):
+        self.gain[...] = self.gain_in[...].astype(F32)[None, :]
         per = self.mean.shape[1]
         for src, dst in ((self.mean, self.mu), (self.rstd, self.rs)):
             for i in range(self.rows // 128):
@@ -259,7 +261,7 @@
         us, xs = [], []
         for k in range(2):
             cols = pl.ds(k * self.hw, self.hw)
-            us.append(sums[k] * self.gain[:, cols].astype(F32))
+            us.append(sums[k] * self.gain[:, cols])
             xs.append((self.zrow[s, :, cols].astype(F32) - mu) * r)
         inv = 1.0 / self.cols
         mean_u = (jnp.sum(us[0], axis=-1, keepdims=True) + jnp.sum(us[1], axis=-1, keepdims=True)) * inv
@@ -309,15 +311,15 @@
     def stages(self):
         x1, x2 = self.l1 * self.hw * 2, self.l2 * self.hw * 2
         return [
-            ('rs1_start', ['pair', 'own'], [('axp', '1+', x1), ('axm', '1-', x1), ('adp', '1+', x1), ('adm', '1-', x1)]),
-            ('rs1_relay', ['axp', 'axm'], [('arp', '1+', x1), ('arm', '1-', x1)]),
+            ('rs1_start', ['pair', 'own'], [('axp', '+', x1), ('axm', '-', x1), ('adp', '+', x1), ('adm', '-', x1)]),
+            ('rs1_relay', ['axp', 'axm'], [('arp', '+', x1), ('arm', '-', x1)]),
             ('rs2_start', ['arp', 'arm', 'adp', 'adm'],
-             [('bxp', '2+', x2), ('bxm', '2-', x2), ('bdp', '2+', x2), ('bdm', '2-', x2)]),
-            ('rs2_relay', ['bxp', 'bxm'], [('brp', '2+', x2), ('brm', '2-', x2)]),
-            ('norm_gather', ['brp', 'brm', 'bdp', 'bdm'], [('csp', '2+', 2 * x2), ('csm', '2-', 2 * x2)]),
-            ('ag2_relay', ['csp', 'csm'], [('cyp', '2+', x2), ('cym', '2-', x2)]),
-            ('ag1_start', ['cyp', 'cym'], [('dsp', '1+', 2 * x1), ('dsm', '1-', 2 * x1), ('k0', 'D', 2 * x1)]),
-            ('ag1_relay', ['dsp', 'dsm'], [('dyp', '1+', x1), ('dym', '1-', x1), ('k3', 'D', 2 * x1), ('k1', 'D', 2 * x1)]),
+             [('bxp', '+', x2), ('bxm', '-', x2), ('bdp', '+', x2), ('bdm', '-', x2)]),
+            ('rs2_relay', ['bxp', 'bxm'], [('brp', '+', x2), ('brm', '-', x2)]),
+            ('norm_gather', ['brp', 'brm', 'bdp', 'bdm'], [('csp', '+', 2 * x2), ('csm', '-', 2 * x2)]),
+            ('ag2_relay', ['csp', 'csm'], [('cyp', '+', x2), ('cym', '-', x2)]),
+            ('ag1_start', ['cyp', 'cym'], [('dsp', '+', 2 * x1), ('dsm', '-', 2 * x1), ('k0', 'D', 2 * x1)]),
+            ('ag1_relay', ['dsp', 'dsm'], [('dyp', '+', x1), ('dym', '-', x1), ('k3', 'D', 2 * x1), ('k1', 'D', 2 * x1)]),
             ('ag1_final', ['dyp', 'dym'], [('k2', 'D', 2 * x1)]),
             ('finish', ['k0', 'k1', 'k2', 'k3'], []),
         ]
@@ -391,9 +393,9 @@
     grid = n_tiles + n_cols
     points = []
     for i in range(n_tiles):
-        points += [(1.6, []), (1.2, []), (1.2, [(i // 2, 'pair' if i % 2 == 0 else 'own')])]
+        points += [(1.1 if i else 5.0, []), (0.7, []), (1.4, [(i // 2, 'pair' if i % 2 == 0 else 'own')])]
     for i in range(n_cols):
-        points += [(0.6, []), (0.8, []), (0.8, [])]
+        points += [(0.5, []), (0.7, []), (0.6, [])]
     plans = comm.plan(points)
 
     def kernel(h1_tile, dy_tile, h1_col, dy_col, w1, w2, mean_ref, rstd_ref, gain_ref, h1_all, dy_all,
@@ -424,7 +426,7 @@
         @pl.when(i < n_tiles)
         def _():
             z = (h1_tile[...].astype(F32) - comm.mu[trow, 0:1]) * comm.rs[trow, 0:1]
-            n2 = (z * gain_ref[...]).astype(BF16)
+            n2 = (z * comm.gain[...]).astype(BF16)
             pre_ref[...] = dot(n2, w1[...])
         ticks(first, 0)
 
@@ -454,7 +456,7 @@
         def _():
             c0 = pl.multiple_of((i - n_tiles) * cb, cb)
             z = (h1_col[...].astype(F32) - comm.mu[:, 0:1]) * comm.rs[:, 0:1]
-            comm.n2c[...] = (z * gain_ref[:, pl.ds(c0, cb)]).astype(BF16)
+            comm.n2c[...] = (z * comm.gain[:, pl.ds(c0, cb)]).astype(BF16)
         ticks(rest, 0)
 
         @pl.when(i >= n_tiles)
@@ -508,8 +510,9 @@
 def attention_stage(n, mbs, x, dh1, mean, rstd, gain, w_qkv, w_out, score_scale, cid):
     rows, cols = x.shape
     seq = rows // mbs
-    hd = w_out.shape[0]
-    qkv_w = w_qkv.shape[1]
+    width = w_out.shape[0]
+    hd = width + -width % 128
+    qkv_w = 3 * hd
     comm = Comm(n, rows, cols)
     tile = comm.half
     per_mb = seq // tile
@@ -519,16 +522,16 @@
     grid = n_seq + n_cols
     points = []
     for b in range(mbs):
-        points += [(1.4, []), (0.4, []), (0.4, [])] * per_mb
+        points += [(1.1 if b else 2.0, []), (0.4, []), (0.1, [])] * per_mb
         for j in range(per_mb - 1, -1, -1):
             s = b * (per_mb // 2) + j // 2
-            points += [(1.4, []), (1.4, []), (1.2, [(s, 'pair'), (s, 'own')] if j % 2 == 0 else [])]
+            points += [(0.8, []), (0.7, []), (1.1, [(s, 'pair'), (s, 'own')] if j % 2 == 0 else [])]
     for i in range(n_cols):
-        points += [(0.7, []), (0.8, []), (0.6, [])]
+        points += [(0.5, []), (0.7, []), (0.4, [])]
     plans = comm.plan(points)
 
-    def kernel(x_tile, dh_tile, x_col, dh_col, wqkv, wo, mean_ref, rstd_ref, gain_ref, x_all, dh_all,
-               dx_ref, dwqkv_ref, dwo_ref, qkv, do, o_all, dqkv, dk_acc, dv_acc, n1c, p_ref, *scratch):
+    def kernel(x_tile, dh_tile, x_col, dh_col, wqkv_in, wo_in, mean_ref, rstd_ref, gain_ref, x_all, dh_all,
+               dx_ref, dwqkv_ref, dwo_ref, qkv, do, o_all, dqkv, dk_acc, dv_acc, n1c, p_ref, wqkv, wo, wsem, *scratch):
         comm.bind(None, x_all, dh_all, mean_ref, rstd_ref, gain_ref, dx_ref, scratch)
         i = pl.program_id(0)
         full, own = comm.full, comm.own
@@ -544,7 +547,18 @@
 
         @pl.when(i == 0)
         def _():
+            loads = [pltpu.make_async_copy(wqkv_in.at[pl.ds(c * width, width), :], wqkv.at[pl.ds(c * hd, width), :],
+                                           wsem.at[c]) for c in range(3)]
+            loads.append(pltpu.make_async_copy(wo_in, wo.at[pl.ds(0, width), :], wsem.at[3]))
+            for load in loads:
+                load.start()
+            zero = jnp.zeros((hd - width, cols), BF16)
+            for c in range(3):
+                wqkv[pl.ds(c * hd + width, hd - width), :] = zero
+            wo[pl.ds(width, hd - width), :] = zero
             comm.begin()
+            for load in loads:
+                load.wait()
 
         span = 2 * per_mb
         first = range(n_seq)
@@ -559,8 +573,8 @@
         @pl.when(loading)
         def _():
             z = (x_tile[...].astype(F32) - comm.mu[trow, 0:1]) * comm.rs[trow, 0:1]
-            n1 = (z * gain_ref[...]).astype(BF16)
-            qkv[trow, :] = dot(n1, wqkv[...]).astype(BF16)
+            n1 = (z * comm.gain[...]).astype(BF16)
+            qkv[trow, :] = dot(n1, wqkv[...], 1, 1).astype(BF16)
 
         def variants(fn):
             for j in range(per_mb):
@@ -606,7 +620,7 @@
 
         def part_c(j):
             mine = pl.ds(pl.multiple_of(base + j * tile, tile), tile)
-            part = dot(dqkv[mine, :], wqkv[...], 1, 1).astype(BF16)
+            part = dot(dqkv[mine, :], wqkv[...]).astype(BF16)
 
             @pl.when(comm.core == j % 2)
             def _():
@@ -632,12 +646,12 @@
         def _():
             c0 = pl.multiple_of((i - n_seq) * cb, cb)
             z = (x_col[...].astype(F32) - comm.mu[:, 0:1]) * comm.rs[:, 0:1]
-            n1c[...] = (z * gain_ref[:, pl.ds(c0, cb)]).astype(BF16)
+            n1c[...] = (z * comm.gain[:, pl.ds(c0, cb)]).astype(BF16)
         ticks(rest, 0)
 
         @pl.when(i >= n_seq)
         def _():
-            dwqkv_ref[...] = dot(n1c[...], dqkv[...], 0, 0).astype(BF16)
+            dwqkv_ref[...] = dot(dqkv[...], n1c[...], 0, 0).astype(BF16)
         ticks(rest, 1)
 
         @pl.when(i >= n_seq)
@@ -661,37 +675,63 @@
     return pl.pallas_call(
         kernel,
         grid=(grid,),
-        out_shape=(jax.ShapeDtypeStruct((rows, cols), BF16), jax.ShapeDtypeStruct((cols, qkv_w), BF16),
+        out_shape=(jax.ShapeDtypeStruct((rows, cols), BF16), jax.ShapeDtypeStruct((qkv_w, cols), BF16),
                    jax.ShapeDtypeStruct((hd, cols), BF16)),
         in_specs=[pl.BlockSpec((tile, cols), tile_map), pl.BlockSpec((tile, cols), tile_map),
                   pl.BlockSpec((rows, cb), lambda i: (0, col_at(i))), pl.BlockSpec((rows, cb), lambda i: (0, col_at(i))),
-                  whole, whole, whole, whole, whole, hbm, hbm],
-        out_specs=(hbm, pl.BlockSpec((cb, qkv_w), lambda i: (col_at(i), 0)),
+                  hbm, hbm, whole, whole, whole, hbm, hbm],
+        out_specs=(hbm, pl.BlockSpec((qkv_w, cb), lambda i: (0, col_at(i))),
                    pl.BlockSpec((hd, cb), lambda i: (0, col_at(i)))),
         scratch_shapes=[VMEM((rows, qkv_w), BF16), VMEM((rows, hd), BF16), VMEM((rows, hd), BF16),
                         VMEM((rows, qkv_w), BF16), VMEM((seq, hd), F32), VMEM((seq, hd), F32), VMEM((rows, cb), BF16),
-                        VMEM((tile, seq), F32)] + comm.scratch(),
+                        VMEM((tile, seq), F32), VMEM((qkv_w, cols), BF16), VMEM((hd, cols), BF16),
+                        pltpu.SemaphoreType.DMA((4,))] + comm.scratch(),
         compiler_params=pltpu.CompilerParams(collective_id=cid, has_side_effects=True, vmem_limit_bytes=VMEM_LIMIT,
                                              dimension_semantics=('arbitrary',)),
         name='attention_stage',
     )(x, dh1, x, dh1, w_qkv, w_out, mean, rstd, gain, x, dh1)
 
 
-def spread_copy(arr):
-    rows, cols = arr.shape
-    tile = 256
-
-    def kernel(src, dst):
-        dst[...] = src[...]
-
+def spread_copy(dx, dw_up, dw_down, dw_qkv, dw_out, width):
+    def rows_of(arr, parts):
+        step = arr.shape[0] // parts
+        return [(k * step, k * step, step) for k in range(parts)]
+
+    hd = dw_out.shape[0]
+    srcs = (dx, dw_up, dw_down, dw_qkv, dw_out)
+    moves = (rows_of(dx, 8), rows_of(dw_up, 2), rows_of(dw_down, 2), [(c * hd, c * width, width) for c in range(3)],
+             [(0, 0, width)])
+    outs = [jax.ShapeDtypeStruct((sum(m[2] for m in mv), a.shape[1]), a.dtype) for a, mv in zip(srcs, moves)]
+    total = sum(len(mv) for mv in moves)
+
+    def kernel(*refs):
+        ins, dsts, bufs, (in_sem, out_sem) = refs[:5], refs[5:10], refs[10:15], refs[15:]
+        reads, writes = [], []
+        for a, mv in enumerate(moves):
+            for frm, to, size in mv:
+                k = len(reads)
+                here = bufs[a].at[pl.ds(to, size), :]
+                reads.append(pltpu.make_async_copy(ins[a].at[pl.ds(frm, size), :], here, in_sem.at[k]))
+                writes.append(pltpu.make_async_copy(here, dsts[a].at[pl.ds(to, size), :], out_sem.at[k]))
+        for read in reads:
+            read.start()
+        for read, write in zip(reads, writes):
+            read.wait()
+            write.start()
+        for write in writes:
+            write.wait()
+
+    hbm = pl.BlockSpec(memory_space=ANY)
     return pl.pallas_call(
         kernel,
-        grid=(rows // tile,),
-        out_shape=jax.ShapeDtypeStruct(arr.shape, arr.dtype),
-        in_specs=[pl.BlockSpec((tile, cols), lambda i: (i, 0))],
-        out_specs=pl.BlockSpec((tile, cols), lambda i: (i, 0)),
+        out_shape=outs,
+        in_specs=[hbm] * 5,
+        out_specs=[hbm] * 5,
+        scratch_shapes=[VMEM(o.shape, o.dtype) for o in outs]
+        + [pltpu.SemaphoreType.DMA((total,)), pltpu.SemaphoreType.DMA((total,))],
+        compiler_params=pltpu.CompilerParams(vmem_limit_bytes=VMEM_LIMIT),
         name='spread_copy',
-    )(arr)
+    )(*srcs)
 
 
 def solution(mesh):
@@ -708,17 +748,15 @@
         score_scale = w_qkv.shape[3] ** -0.5
         shape = x_saved.shape
         flat = (shape[0] * shape[1], shape[2])
-        g1, g2 = gain_one.astype(F32)[None, :], gain_two.astype(F32)[None, :]
+        g1, g2 = gain_one, gain_two
         dh1, grad_up, grad_down = mlp_stage(n, h1_saved.reshape(flat), grad_y.reshape(flat), mean_two, rstd_two, g2,
                                             w_up, w_down, 0)
         heads, _, width = w_qkv.shape[1:]
-        pad = -width % 128
-        wide_qkv = jnp.pad(w_qkv[:, 0], ((0, 0), (0, 0), (0, pad))).reshape(flat[1], -1)
-        wide_out = jnp.pad(w_out[0], ((0, pad), (0, 0)))
+        rows_qkv = w_qkv.transpose(1, 2, 3, 0).reshape(3 * width, flat[1])
         dx, dqkv_w, dout_w = attention_stage(n, shape[0], x_saved.reshape(flat), dh1, mean_one, rstd_one, g1,
-                                             wide_qkv, wide_out, score_scale, 1)
-        grad_qkv_w = dqkv_w.reshape(flat[1], heads, 3, width + pad)[..., :width]
-        grad_out_w = dout_w[None, :width]
-        return spread_copy(dx).reshape(shape), grad_qkv_w, grad_out_w, grad_up, grad_down
+                                             rows_qkv, w_out[0], score_scale, 1)
+        dx, grad_up, grad_down, dqkv_w, dout_w = spread_copy(dx, grad_up, grad_down, dqkv_w, dout_w, width)
+        grad_qkv_w = dqkv_w.reshape(heads, 3, width, flat[1]).transpose(3, 0, 1, 2)
+        return dx.reshape(shape), grad_qkv_w, dout_w[None], grad_up, grad_down
 
     return jax.shard_map(local_backward, mesh=mesh, in_specs=in_specs, out_specs=out_specs, check_vma=False)

time: 252 us -> 241 us (0.956)
  local copies, waits for them, and re-layouts: 16.1 us -> 0 us
  Pallas kernels: 232 us -> 240 us
  other arithmetic: 2.59 us -> 0 us
    pallas_call x1, Pallas kernels: 101 us -> 114 us  [mlp_stage(): pl.pallas_call(wrapped, grid=(grid,), out_shape=(jax.ShapeDtypeStruct((ro...]
    pallas_call x1, Pallas kernels: 119 us -> 112 us  [attention_stage(): pl.pallas_call(kernel, grid=(grid,), out_shape=(jax.ShapeDtypeStruct((row...]
    unnamed x8 -> x0, local copies, waits for them, and re-layouts: 4.9 us -> none
    pad x2 -> x0, local copies, waits for them, and re-layouts: 3.73 us -> none  [the longest x1 2.01 us: local_backward(): wide_out = jnp.pad(w_out[0], ((0, pad), (0, 0)))]
    pallas_call x1 -> x0, local copies, waits for them, and re-layouts: 2.83 us -> none  [attention_stage(): pl.pallas_call(kernel, grid=(grid,), out_shape=(jax.ShapeDtypeStruct((row...]
    broadcast_in_dim x2 -> x0, other arithmetic: 2.59 us -> none  [local_backward(): g1, g2 = (gain_one.astype(F32)[None, :], gain_two.astype(F32)[None, :])]
where the time goes in v2:
time: 241 us
  Pallas kernels  240 us (100%)
    pallas_call x1, Pallas kernels, mlp_stage(): pl.pallas_call(wrapped, grid=(grid,), out_shape=(jax.ShapeDtypeStruct((ro...  114 us
    pallas_call x1, Pallas kernels, attention_stage(): pl.pallas_call(kernel, grid=(grid,), out_shape=(jax.ShapeDtypeStruct((row...  112 us
    pallas_call x1, Pallas kernels, spread_copy(): pl.pallas_call(kernel, out_shape=outs, in_specs=[hbm] * 5, out_specs=[hbm...  13.9 us

profile of v2, /device:TPU:97, one launch (start us, length us, event | category | flops | bytes accessed | tf_op | source)
XLA Modules:
  0.0 240.9 jit_solution(18148559386283522783)
XLA Ops:
  0.6 113.7 %mlp_stage.1 = (bf16[2048,3072]{1,0:T(8,128)(2,1)}, bf16[3072,384]{1,0:T(8,128)(2,1)}, bf16[384,3072]{1,0:T(8,128)(2,1)}) custom-call(bf16[2048,3072]{1,0:T(8,128)(2,1)} %bitcast.12, bf16[2048,3072]{1,0:T(8,128)(2,1)} %bitcast.15, bf16[2048,3072]{1,0:T(8,128)(2,1)} %bitcast.13, bf16[2048,3072]{1,0:T(8,128)(2,1)} %bitcast.16, bf16[3072,384]{1,0:T(8,128)(2,1)} %refs_4_.1, ...), custom_call_target="tpu_custom_call" | custom-call | tf_op jit(solution)/shard_map/mlp_stage/pallas_call | solution.py:492
  114.3 112.5 %attention_stage.1 = (bf16[2048,3072]{1,0:T(8,128)(2,1)}, bf16[384,3072]{1,0:T(8,128)(2,1)}, bf16[128,3072]{1,0:T(8,128)(2,1)}) custom-call(bf16[2048,3072]{1,0:T(8,128)(2,1)} %bitcast.18, bf16[2048,3072]{1,0:T(8,128)(2,1)} %get-tuple-element.16.dh_tile.dh_col.dh_all, bf16[2048,3072]{1,0:T(8,128)(2,1)} %bitcast.19, ...), custom_call_target="tpu_custom_call" | custom-call | tf_op jit(solution)/shard_map/attention_stage/pallas_call | solution.py:675
  226.8 13.9 %spread_copy.1 = (bf16[2048,3072]{1,0:T(8,128)(2,1)}, bf16[3072,384]{1,0:T(8,128)(2,1)}, bf16[384,3072]{1,0:T(8,128)(2,1)}, bf16[288,3072]{1,0:T(8,128)(2,1)}, bf16[96,3072]{1,0:T(8,128)(2,1)}) custom-call(bf16[2048,3072]{1,0:T(8,128)(2,1)} %get-tuple-element.17.refs_0_, bf16[3072,384]{1,0:T(8,128)(2,1)} %get-tuple-element.18.refs_1_, ...), custom_call_target="tpu_custom_call" | custom-call | tf_op jit(solution)/shard_map/spread_copy/pallas_call | solution.py:725

commit v3 on v2

--- a/solution.py
+++ b/solution.py
@@ -58,7 +58,6 @@
             VMEM((ns, l2, w), BF16),
             VMEM((ns, l2, w), BF16),
             VMEM((self.rows, 128), F32),
-            VMEM((self.rows, 128), F32),
             VMEM((1, w), F32),
             pltpu.SemaphoreType.DMA((ns, SEMS)),
             pltpu.SemaphoreType.DMA((ns, SEMS)),
@@ -66,11 +65,11 @@
             pltpu.SemaphoreType.REGULAR((ns,)),
         ]
 
-    def bind(self, part, saved, resid, mean, rstd, gain, out, scratch):
-        (self.own, self.pair, self.ring1, self.ring2, self.full, self.zrow, self.rrow, self.mu, self.rs, self.gain,
+    def bind(self, part, saved, resid, stats, gain, out, scratch):
+        (self.own, self.pair, self.ring1, self.ring2, self.full, self.zrow, self.rrow, self.cols_of, self.gain,
          self.ssem, self.rsem, self.lsem, self.freed) = scratch
         self.part, self.saved, self.resid, self.gain_in, self.out = part, saved, resid, gain, out
-        self.mean, self.rstd = mean, rstd
+        self.stats = stats
         side = self.side
         me = lax.axis_index('tp')
         core = lax.rem(me, 2)
@@ -185,12 +184,17 @@
 
     def columns(self):
         self.gain[...] = self.gain_in[...].astype(F32)[None, :]
-        per = self.mean.shape[1]
-        for src, dst in ((self.mean, self.mu), (self.rstd, self.rs)):
-            for i in range(self.rows // 128):
-                b, off = divmod(i * 128, per)
-                row = src[b:b + 1, off:off + 128]
-                dst[pl.ds(i * 128, 128), :] = jnp.transpose(jnp.broadcast_to(row, (128, 128)))
+        per = self.stats[0].shape[1]
+        lane = lax.broadcasted_iota(jnp.int32, (128, 128), 0)
+        for i in range(self.rows // 128):
+            b, off = divmod(i * 128, per)
+            block = jnp.zeros((128, 128), F32)
+            for k, src in enumerate(self.stats):
+                block = jnp.where(lane == k, jnp.broadcast_to(src[b:b + 1, off:off + 128], (128, 128)), block)
+            self.cols_of[pl.ds(i * 128, 128), :] = jnp.transpose(block)
+
+    def normed(self, block, rows, k):
+        return (block.astype(F32) - self.cols_of[rows, k:k + 1]) * self.cols_of[rows, k + 1:k + 2]
 
     def begin(self):
         for s in range(self.streams):
@@ -256,8 +260,8 @@
         self.local(s, 1).wait()
         self.local(s, 2).wait()
         mine = self.mine(s)
-        mu = self.mu[mine, 0:1]
-        r = self.rs[mine, 0:1]
+        mu = self.cols_of[mine, 0:1]
+        r = self.cols_of[mine, 1:2]
         us, xs = [], []
         for k in range(2):
             cols = pl.ds(k * self.hw, self.hw)
@@ -369,12 +373,32 @@
         self.estimate = now
         return plans
 
+    def tuned(self, table, points):
+        self.points = points
+        plans = self.plan(points)
+        if not table or len(plans) != table[0]:
+            return plans
+        names = [stage[0] for stage in self.stages()]
+        out = [[step for step in todo if step[0] == 'send_pair'] for todo in plans]
+        for code in table[1]:
+            point, rest = divmod(code, 64)
+            out[point].append((names[rest // 4], rest % 4))
+        return out
+
     def send_pair(self, s):
         self.start(s, 'pair')
 
     part_given = False
 
 
+MLP_PLAN = (84, [
+    448, 769, 965, 964, 1161, 1154, 1352, 1357, 1414, 1539, 1863, 1868, 1873, 1866, 2187, 2261, 2318, 2383,
+    2384, 2457, 2706, 2899, 2900, 2909, 3030, 3096, 3351, 3418, 3740, 3931, 4190, 4256, 4639, 4834, 4833,
+    5155, 5220, 5349, 5350, 5351])
+ATT_PLAN = (84, [
+    1409, 1989, 2441, 2432, 2701, 2692, 2833, 2883, 3016, 3015, 3020, 3074, 3280, 3398, 3541, 3668, 3659,
+    3722, 3737, 3918, 3919, 4056, 4306, 4307, 4316, 4374, 4445, 4439, 4634, 4827, 4832, 4897, 4894, 5092,
+    5151, 5282, 5349, 5347, 5350, 5351])
 VMEM_LIMIT = 64 * 1024 * 1024 - 64 * 1024
 
 
@@ -382,7 +406,7 @@
     return lax.dot_general(a, b, (((ca,), (cb,)), ((), ())), preferred_element_type=F32)
 
 
-def mlp_stage(n, h1, dy, mean, rstd, gain, w_up, w_down, cid):
+def mlp_stage(n, h1, dy, x, stats, gain, gain_x, w_up, w_down, w_qkv, width, cid):
     rows, cols = h1.shape
     ffn = w_up.shape[1]
     comm = Comm(n, rows, cols)
@@ -390,17 +414,21 @@
     n_tiles = rows // tile
     cb = 256
     n_cols = cols // cb
-    grid = n_tiles + n_cols
+    hd = width + -width % 128
+    qkv_w = 3 * hd
+    dw_end = n_tiles + n_cols
+    grid = dw_end + n_tiles
     points = []
     for i in range(n_tiles):
-        points += [(1.1 if i else 5.0, []), (0.7, []), (1.4, [(i // 2, 'pair' if i % 2 == 0 else 'own')])]
+        points += [(1.5 if i else 7.0, []), (0.9, []), (2.0, [(i // 2, 'pair' if i % 2 == 0 else 'own')])]
     for i in range(n_cols):
-        points += [(0.5, []), (0.7, []), (0.6, [])]
-    plans = comm.plan(points)
-
-    def kernel(h1_tile, dy_tile, h1_col, dy_col, w1, w2, mean_ref, rstd_ref, gain_ref, h1_all, dy_all,
-               dh1_ref, dw1_ref, dw2_ref, act, da, *scratch):
-        comm.bind(None, h1_all, dy_all, mean_ref, rstd_ref, gain_ref, dh1_ref, scratch)
+        points += [(0.6, []), (1.0, []), (0.85, [])]
+    points += [(1.6, []), (0.0, []), (0.0, [])] * n_tiles
+    plans = comm.tuned(MLP_PLAN, points)
+
+    def kernel(h1_tile, dy_tile, h1_col, dy_col, x_tile, w1, w2, mean2, rstd2, mean1, rstd1, gain_ref, gain_x_ref,
+               wqkv_in, h1_all, dy_all, dh1_ref, dw1_ref, dw2_ref, qkv_ref, act, da, wqkv, gx, wsem, *scratch):
+        comm.bind(None, h1_all, dy_all, (mean2, rstd2, mean1, rstd1), gain_ref, dh1_ref, scratch)
         i = pl.program_id(0)
         full, own = comm.full, comm.own
 
@@ -413,20 +441,28 @@
                         for name, s in todo:
                             getattr(comm, name)(s)
 
+        loads = [pltpu.make_async_copy(wqkv_in.at[pl.ds(c * width, width), :], wqkv.at[pl.ds(c * hd, width), :],
+                                       wsem.at[c]) for c in range(3)]
+
         @pl.when(i == 0)
         def _():
+            for load in loads:
+                load.start()
+            for c in range(3):
+                wqkv[pl.ds(c * hd + width, hd - width), :] = jnp.zeros((hd - width, cols), BF16)
+            gx[...] = gain_x_ref[...].astype(F32)[None, :]
             comm.begin()
 
         first = range(n_tiles)
-        rest = range(n_tiles, grid)
+        rest = range(n_tiles, dw_end)
+        last = range(dw_end, grid)
         tidx = lax.div(i, 2) * 2 + lax.rem(i, 2) * comm.core + (1 - lax.rem(i, 2)) * (1 - comm.core)
         trow = pl.ds(pl.multiple_of(tidx * tile, tile), tile)
         pre_ref, dg_ref = comm.pre, comm.dg
 
         @pl.when(i < n_tiles)
         def _():
-            z = (h1_tile[...].astype(F32) - comm.mu[trow, 0:1]) * comm.rs[trow, 0:1]
-            n2 = (z * comm.gain[...]).astype(BF16)
+            n2 = (comm.normed(h1_tile[...], trow, 0) * comm.gain[...]).astype(BF16)
             pre_ref[...] = dot(n2, w1[...])
         ticks(first, 0)
 
@@ -452,22 +488,35 @@
                 own[lax.div(i, 2)] = part
         ticks(first, 2)
 
-        @pl.when(i >= n_tiles)
+        @pl.when(jnp.logical_and(i >= n_tiles, i < dw_end))
         def _():
             c0 = pl.multiple_of((i - n_tiles) * cb, cb)
-            z = (h1_col[...].astype(F32) - comm.mu[:, 0:1]) * comm.rs[:, 0:1]
-            comm.n2c[...] = (z * comm.gain[:, pl.ds(c0, cb)]).astype(BF16)
+            comm.n2c[...] = (comm.normed(h1_col[...], pl.ds(0, rows), 0) * comm.gain[:, pl.ds(c0, cb)]).astype(BF16)
         ticks(rest, 0)
 
-        @pl.when(i >= n_tiles)
+        @pl.when(jnp.logical_and(i >= n_tiles, i < dw_end))
         def _():
             dw1_ref[...] = dot(comm.n2c[...], da[...], 0, 0).astype(BF16)
         ticks(rest, 1)
 
-        @pl.when(i >= n_tiles)
+        @pl.when(jnp.logical_and(i >= n_tiles, i < dw_end))
         def _():
             dw2_ref[...] = dot(act[...], dy_col[...], 0, 0).astype(BF16)
         ticks(rest, 2)
+
+        @pl.when(i == dw_end)
+        def _():
+            for load in loads:
+                load.wait()
+
+        @pl.when(i >= dw_end)
+        def _():
+            xrow = pl.ds(pl.multiple_of((i - dw_end) * tile, tile), tile)
+            n1 = (comm.normed(x_tile[...], xrow, 2) * gx[...]).astype(BF16)
+            qkv_ref[...] = dot(n1, wqkv[...], 1, 1).astype(BF16)
+        ticks(last, 0)
+        ticks(last, 1)
+        ticks(last, 2)
 
         @pl.when(i == grid - 1)
         def _():
@@ -485,7 +534,10 @@
         return lax.div(ii, 2) * 2 + odd * core + (1 - odd) * (1 - core), 0
 
     def col_at(i):
-        return jnp.maximum(i - n_tiles, 0)
+        return jnp.clip(i - n_tiles, 0, n_cols - 1)
+
+    def x_at(i):
+        return jnp.maximum(i - dw_end, 0), 0
 
     whole = pl.BlockSpec(memory_space=VMEM)
     hbm = pl.BlockSpec(memory_space=ANY)
@@ -493,21 +545,22 @@
         wrapped,
         grid=(grid,),
         out_shape=(jax.ShapeDtypeStruct((rows, cols), BF16), jax.ShapeDtypeStruct((cols, ffn), BF16),
-                   jax.ShapeDtypeStruct((ffn, cols), BF16)),
+                   jax.ShapeDtypeStruct((ffn, cols), BF16), jax.ShapeDtypeStruct((rows, qkv_w), BF16)),
         in_specs=[pl.BlockSpec((tile, cols), tile_map), pl.BlockSpec((tile, cols), tile_map),
                   pl.BlockSpec((rows, cb), lambda i: (0, col_at(i))), pl.BlockSpec((rows, cb), lambda i: (0, col_at(i))),
-                  whole, whole, whole, whole, whole, hbm, hbm],
+                  pl.BlockSpec((tile, cols), x_at), whole, whole] + [whole] * 6 + [hbm] * 3,
         out_specs=(hbm, pl.BlockSpec((cb, ffn), lambda i: (col_at(i), 0)),
-                   pl.BlockSpec((ffn, cb), lambda i: (0, col_at(i)))),
-        scratch_shapes=[VMEM((rows, ffn), BF16), VMEM((rows, ffn), BF16)] + comm.scratch()
+                   pl.BlockSpec((ffn, cb), lambda i: (0, col_at(i))), pl.BlockSpec((tile, qkv_w), x_at)),
+        scratch_shapes=[VMEM((rows, ffn), BF16), VMEM((rows, ffn), BF16), VMEM((qkv_w, cols), BF16), VMEM((1, cols), F32),
+                        pltpu.SemaphoreType.DMA((3,))] + comm.scratch()
         + [VMEM((tile, ffn), F32), VMEM((tile, ffn), F32), VMEM((rows, cb), BF16)],
         compiler_params=pltpu.CompilerParams(collective_id=cid, has_side_effects=True, vmem_limit_bytes=VMEM_LIMIT,
                                              dimension_semantics=('arbitrary',)),
         name='mlp_stage',
-    )(h1, dy, h1, dy, w_up, w_down, mean, rstd, gain, h1, dy)
-
-
-def attention_stage(n, mbs, x, dh1, mean, rstd, gain, w_qkv, w_out, score_scale, cid):
+    )(h1, dy, h1, dy, x, w_up, w_down, *stats, gain, gain_x, w_qkv, h1, dy)
+
+
+def attention_stage(n, mbs, x, dh1, qkv_all, stats, gain, w_qkv, w_out, score_scale, cid):
     rows, cols = x.shape
     seq = rows // mbs
     width = w_out.shape[0]
@@ -522,17 +575,18 @@
     grid = n_seq + n_cols
     points = []
     for b in range(mbs):
-        points += [(1.1 if b else 2.0, []), (0.4, []), (0.1, [])] * per_mb
+        points += [(0.0, []), (0.8, []), (0.0, [])] * per_mb
         for j in range(per_mb - 1, -1, -1):
             s = b * (per_mb // 2) + j // 2
-            points += [(0.8, []), (0.7, []), (1.1, [(s, 'pair'), (s, 'own')] if j % 2 == 0 else [])]
+            points += [(1.0, []), (0.9, []), (1.45, [(s, 'pair'), (s, 'own')] if j % 2 == 0 else [])]
     for i in range(n_cols):
-        points += [(0.5, []), (0.7, []), (0.4, [])]
-    plans = comm.plan(points)
-
-    def kernel(x_tile, dh_tile, x_col, dh_col, wqkv_in, wo_in, mean_ref, rstd_ref, gain_ref, x_all, dh_all,
-               dx_ref, dwqkv_ref, dwo_ref, qkv, do, o_all, dqkv, dk_acc, dv_acc, n1c, p_ref, wqkv, wo, wsem, *scratch):
-        comm.bind(None, x_all, dh_all, mean_ref, rstd_ref, gain_ref, dx_ref, scratch)
+        points += [(0.7, []), (1.0, []), (0.4, [])]
+    points[0] = (5.5, [])
+    plans = comm.tuned(ATT_PLAN, points)
+
+    def kernel(dh_tile, x_col, dh_col, qkv, wqkv_in, wo_in, mean_ref, rstd_ref, gain_ref, x_all, dh_all,
+               dx_ref, dwqkv_ref, dwo_ref, do, o_all, dqkv, dk_acc, dv_acc, n1c, p_ref, wqkv, wo, wsem, *scratch):
+        comm.bind(None, x_all, dh_all, (mean_ref, rstd_ref), gain_ref, dx_ref, scratch)
         i = pl.program_id(0)
         full, own = comm.full, comm.own
 
@@ -569,12 +623,6 @@
         loading = jnp.logical_and(in_seq, at < per_mb)
         base = b * seq
         trow = pl.ds(pl.multiple_of(jnp.minimum(base + at * tile, rows - tile), tile), tile)
-
-        @pl.when(loading)
-        def _():
-            z = (x_tile[...].astype(F32) - comm.mu[trow, 0:1]) * comm.rs[trow, 0:1]
-            n1 = (z * comm.gain[...]).astype(BF16)
-            qkv[trow, :] = dot(n1, wqkv[...], 1, 1).astype(BF16)
 
         def variants(fn):
             for j in range(per_mb):
@@ -645,8 +693,7 @@
         @pl.when(i >= n_seq)
         def _():
             c0 = pl.multiple_of((i - n_seq) * cb, cb)
-            z = (x_col[...].astype(F32) - comm.mu[:, 0:1]) * comm.rs[:, 0:1]
-            n1c[...] = (z * comm.gain[:, pl.ds(c0, cb)]).astype(BF16)
+            n1c[...] = (comm.normed(x_col[...], pl.ds(0, rows), 0) * comm.gain[:, pl.ds(c0, cb)]).astype(BF16)
         ticks(rest, 0)
 
         @pl.when(i >= n_seq)
@@ -677,19 +724,19 @@
         grid=(grid,),
         out_shape=(jax.ShapeDtypeStruct((rows, cols), BF16), jax.ShapeDtypeStruct((qkv_w, cols), BF16),
                    jax.ShapeDtypeStruct((hd, cols), BF16)),
-        in_specs=[pl.BlockSpec((tile, cols), tile_map), pl.BlockSpec((tile, cols), tile_map),
+        in_specs=[pl.BlockSpec((tile, cols), tile_map),
                   pl.BlockSpec((rows, cb), lambda i: (0, col_at(i))), pl.BlockSpec((rows, cb), lambda i: (0, col_at(i))),
-                  hbm, hbm, whole, whole, whole, hbm, hbm],
+                  whole, hbm, hbm, whole, whole, whole, hbm, hbm],
         out_specs=(hbm, pl.BlockSpec((qkv_w, cb), lambda i: (0, col_at(i))),
                    pl.BlockSpec((hd, cb), lambda i: (0, col_at(i)))),
-        scratch_shapes=[VMEM((rows, qkv_w), BF16), VMEM((rows, hd), BF16), VMEM((rows, hd), BF16),
+        scratch_shapes=[VMEM((rows, hd), BF16), VMEM((rows, hd), BF16),
                         VMEM((rows, qkv_w), BF16), VMEM((seq, hd), F32), VMEM((seq, hd), F32), VMEM((rows, cb), BF16),
                         VMEM((tile, seq), F32), VMEM((qkv_w, cols), BF16), VMEM((hd, cols), BF16),
                         pltpu.SemaphoreType.DMA((4,))] + comm.scratch(),
         compiler_params=pltpu.CompilerParams(collective_id=cid, has_side_effects=True, vmem_limit_bytes=VMEM_LIMIT,
                                              dimension_semantics=('arbitrary',)),
         name='attention_stage',
-    )(x, dh1, x, dh1, w_qkv, w_out, mean, rstd, gain, x, dh1)
+    )(dh1, x, dh1, qkv_all, w_qkv, w_out, *stats, gain, x, dh1)
 
 
 def spread_copy(dx, dw_up, dw_down, dw_qkv, dw_out, width):
@@ -748,13 +795,13 @@
         score_scale = w_qkv.shape[3] ** -0.5
         shape = x_saved.shape
         flat = (shape[0] * shape[1], shape[2])
-        g1, g2 = gain_one, gain_two
-        dh1, grad_up, grad_down = mlp_stage(n, h1_saved.reshape(flat), grad_y.reshape(flat), mean_two, rstd_two, g2,
-                                            w_up, w_down, 0)
         heads, _, width = w_qkv.shape[1:]
         rows_qkv = w_qkv.transpose(1, 2, 3, 0).reshape(3 * width, flat[1])
-        dx, dqkv_w, dout_w = attention_stage(n, shape[0], x_saved.reshape(flat), dh1, mean_one, rstd_one, g1,
-                                             rows_qkv, w_out[0], score_scale, 1)
+        h1, dy, x = h1_saved.reshape(flat), grad_y.reshape(flat), x_saved.reshape(flat)
+        dh1, grad_up, grad_down, qkv = mlp_stage(n, h1, dy, x, (mean_two, rstd_two, mean_one, rstd_one), gain_two,
+                                                 gain_one, w_up, w_down, rows_qkv, width, 0)
+        dx, dqkv_w, dout_w = attention_stage(n, shape[0], x, dh1, qkv, (mean_one, rstd_one), gain_one, rows_qkv,
+                                             w_out[0], score_scale, 1)
         dx, grad_up, grad_down, dqkv_w, dout_w = spread_copy(dx, grad_up, grad_down, dqkv_w, dout_w, width)
         grad_qkv_w = dqkv_w.reshape(heads, 3, width, flat[1]).transpose(3, 0, 1, 2)
         return dx.reshape(shape), grad_qkv_w, dout_w[None], grad_up, grad_down

time: 241 us -> 233 us (0.967)
  Pallas kernels: 240 us -> 232 us
    pallas_call x1, Pallas kernels: 112 us -> 106 us  [attention_stage(): pl.pallas_call(kernel, grid=(grid,), out_shape=(jax.ShapeDtypeStruct((row...]
where the time goes in v3:
time: 233 us
  Pallas kernels  232 us (100%)
    pallas_call x1, Pallas kernels, mlp_stage(): pl.pallas_call(wrapped, grid=(grid,), out_shape=(jax.ShapeDtypeStruct((ro...  113 us
    pallas_call x1, Pallas kernels, attention_stage(): pl.pallas_call(kernel, grid=(grid,), out_shape=(jax.ShapeDtypeStruct((row...  106 us
    pallas_call x1, Pallas kernels, spread_copy(): pl.pallas_call(kernel, out_shape=outs, in_specs=[hbm] * 5, out_specs=[hbm...  13.9 us

profile of v3, /device:TPU:97, one launch (start us, length us, event | category | flops | bytes accessed | tf_op | source)
XLA Modules:
  0.0 233.2 jit_solution(8495979633300087972)
XLA Ops:
  0.6 112.8 %mlp_stage.1 = (bf16[2048,3072]{1,0:T(8,128)(2,1)}, bf16[3072,384]{1,0:T(8,128)(2,1)}, bf16[384,3072]{1,0:T(8,128)(2,1)}, bf16[2048,384]{1,0:T(8,128)(2,1)}) custom-call(bf16[2048,3072]{1,0:T(8,128)(2,1)} %bitcast.12, bf16[2048,3072]{1,0:T(8,128)(2,1)} %bitcast.15, bf16[2048,3072]{1,0:T(8,128)(2,1)} %bitcast.13, bf16[2048,3072]{1,0:T(8,128)(2,1)} %bitcast.16, ...), custom_call_target="tpu_custom_call" | custom-call | tf_op jit(solution)/shard_map/mlp_stage/pallas_call | solution.py:544
  113.5 105.7 %attention_stage.1 = (bf16[2048,3072]{1,0:T(8,128)(2,1)}, bf16[384,3072]{1,0:T(8,128)(2,1)}, bf16[128,3072]{1,0:T(8,128)(2,1)}) custom-call(bf16[2048,3072]{1,0:T(8,128)(2,1)} %get-tuple-element.17.dh_tile.dh_col.dh_all, bf16[2048,3072]{1,0:T(8,128)(2,1)} %bitcast.19, bf16[2048,3072]{1,0:T(8,128)(2,1)} %get-tuple-element.17.dh_tile.dh_col.dh_all, ...), custom_call_target="tpu_custom_call" | custom-call | tf_op jit(solution)/shard_map/attention_stage/pallas_call | solution.py:722
  219.2 13.9 %spread_copy.1 = (bf16[2048,3072]{1,0:T(8,128)(2,1)}, bf16[3072,384]{1,0:T(8,128)(2,1)}, bf16[384,3072]{1,0:T(8,128)(2,1)}, bf16[288,3072]{1,0:T(8,128)(2,1)}, bf16[96,3072]{1,0:T(8,128)(2,1)}) custom-call(bf16[2048,3072]{1,0:T(8,128)(2,1)} %get-tuple-element.19.refs_0_, bf16[3072,384]{1,0:T(8,128)(2,1)} %get-tuple-element.20.refs_1_, ...), custom_call_target="tpu_custom_call" | custom-call | tf_op jit(solution)/shard_map/spread_copy/pallas_call | solution.py:772

commit v4 on v3

--- a/solution.py
+++ b/solution.py
@@ -50,7 +50,6 @@
     def scratch(self):
         l1, l2, w, hw, ns = self.l1, self.l2, self.cols, self.hw, self.streams
         return [
-            VMEM((ns, self.half, w), BF16),
             VMEM((ns, self.half, w), BF16),
             VMEM((ns, 6, l1, hw), BF16),
             VMEM((ns, 6, l2, hw), BF16),
@@ -66,7 +65,7 @@
         ]
 
     def bind(self, part, saved, resid, stats, gain, out, scratch):
-        (self.own, self.pair, self.ring1, self.ring2, self.full, self.zrow, self.rrow, self.cols_of, self.gain,
+        (self.own, self.ring1, self.ring2, self.full, self.zrow, self.rrow, self.cols_of, self.gain,
          self.ssem, self.rsem, self.lsem, self.freed) = scratch
         self.part, self.saved, self.resid, self.gain_in, self.out = part, saved, resid, gain, out
         self.stats = stats
@@ -107,8 +106,8 @@
         own, full = self.own.at[s], self.full
         row0 = s * self.blk
         out = {}
-        source = self.full if self.part is None else self.part
-        out['pair'] = (0, source.at[self.half_rows(s, 1), :], self.pair.at[s], self.partner)
+        theirs = full.at[self.half_rows(s, 1), :]
+        out['pair'] = (0, theirs, theirs, self.partner)
 
         def ring(tag, first, base, size, p, bufs, devs):
             plus, minus = devs
@@ -216,7 +215,8 @@
 
         def add(i, carry):
             rows = pl.ds(pl.multiple_of(i * step, step), step)
-            self.own[s, rows, :] = (self.own[s, rows, :].astype(F32) + self.pair[s, rows, :].astype(F32)).astype(BF16)
+            got = self.full[self.ds(s * self.blk + self.core * self.half + i * step, step), :]
+            self.own[s, rows, :] = (self.own[s, rows, :].astype(F32) + got.astype(F32)).astype(BF16)
             return carry
 
         lax.fori_loop(0, self.half // step, add, 0)
@@ -391,14 +391,14 @@
     part_given = False
 
 
-MLP_PLAN = (84, [
-    448, 769, 965, 964, 1161, 1154, 1352, 1357, 1414, 1539, 1863, 1868, 1873, 1866, 2187, 2261, 2318, 2383,
-    2384, 2457, 2706, 2899, 2900, 2909, 3030, 3096, 3351, 3418, 3740, 3931, 4190, 4256, 4639, 4834, 4833,
-    5155, 5220, 5349, 5350, 5351])
-ATT_PLAN = (84, [
-    1409, 1989, 2441, 2432, 2701, 2692, 2833, 2883, 3016, 3015, 3020, 3074, 3280, 3398, 3541, 3668, 3659,
-    3722, 3737, 3918, 3919, 4056, 4306, 4307, 4316, 4374, 4445, 4439, 4634, 4827, 4832, 4897, 4894, 5092,
-    5151, 5282, 5349, 5347, 5350, 5351])
+MLP_PLAN = (60, [
+    512, 769, 964, 1029, 1154, 1352, 1417, 1414, 1549, 1539, 1674, 1799, 1934, 1932, 1937, 1995, 2002, 2064,
+    2127, 2133, 2198, 2196, 2195, 2265, 2330, 2653, 2647, 2712, 2846, 2907, 3170, 3169, 3164, 3295, 3365,
+    3488, 3494, 3555, 3684, 3751])
+ATT_PLAN = (54, [
+    1153, 1605, 1664, 1865, 1860, 2061, 2051, 2248, 2247, 2257, 2380, 2370, 2517, 2502, 2507, 2576, 2634,
+    2639, 2649, 2766, 2771, 2836, 2845, 2834, 2903, 2904, 2977, 3030, 3035, 3098, 3167, 3228, 3294, 3363,
+    3424, 3426, 3429, 3428, 3431, 3430])
 VMEM_LIMIT = 64 * 1024 * 1024 - 64 * 1024
 
 
@@ -412,18 +412,19 @@
     comm = Comm(n, rows, cols)
     tile = comm.half
     n_tiles = rows // tile
-    cb = 256
+    cb = 384
     n_cols = cols // cb
     hd = width + -width % 128
     qkv_w = 3 * hd
     dw_end = n_tiles + n_cols
-    grid = dw_end + n_tiles
+    wide = 2 * tile
+    grid = dw_end + rows // wide
     points = []
     for i in range(n_tiles):
         points += [(1.5 if i else 7.0, []), (0.9, []), (2.0, [(i // 2, 'pair' if i % 2 == 0 else 'own')])]
     for i in range(n_cols):
-        points += [(0.6, []), (1.0, []), (0.85, [])]
-    points += [(1.6, []), (0.0, []), (0.0, [])] * n_tiles
+        points += [(1.0, []), (1.5, []), (1.2, [])]
+    points += [(2.8, []), (0.0, []), (0.0, [])] * (rows // wide)
     plans = comm.tuned(MLP_PLAN, points)
 
     def kernel(h1_tile, dy_tile, h1_col, dy_col, x_tile, w1, w2, mean2, rstd2, mean1, rstd1, gain_ref, gain_x_ref,
@@ -433,13 +434,16 @@
         full, own = comm.full, comm.own
 
         def ticks(steps, k):
-            for step in steps:
-                todo = plans[step * 3 + k]
-                if todo:
-                    @pl.when(i == step)
-                    def _():
-                        for name, s in todo:
-                            getattr(comm, name)(s)
+            if any(plans[step * 3 + k] for step in steps):
+                @pl.when(jnp.logical_and(i >= steps[0], i <= steps[-1]))
+                def _():
+                    for step in steps:
+                        todo = plans[step * 3 + k]
+                        if todo:
+                            @pl.when(i == step)
+                            def _():
+                                for name, s in todo:
+                                    getattr(comm, name)(s)
 
         loads = [pltpu.make_async_copy(wqkv_in.at[pl.ds(c * width, width), :], wqkv.at[pl.ds(c * hd, width), :],
                                        wsem.at[c]) for c in range(3)]
@@ -511,7 +515,7 @@
 
         @pl.when(i >= dw_end)
         def _():
-            xrow = pl.ds(pl.multiple_of((i - dw_end) * tile, tile), tile)
+            xrow = pl.ds(pl.multiple_of((i - dw_end) * wide, wide), wide)
             n1 = (comm.normed(x_tile[...], xrow, 2) * gx[...]).astype(BF16)
             qkv_ref[...] = dot(n1, wqkv[...], 1, 1).astype(BF16)
         ticks(last, 0)
@@ -548,9 +552,9 @@
                    jax.ShapeDtypeStruct((ffn, cols), BF16), jax.ShapeDtypeStruct((rows, qkv_w), BF16)),
         in_specs=[pl.BlockSpec((tile, cols), tile_map), pl.BlockSpec((tile, cols), tile_map),
                   pl.BlockSpec((rows, cb), lambda i: (0, col_at(i))), pl.BlockSpec((rows, cb), lambda i: (0, col_at(i))),
-                  pl.BlockSpec((tile, cols), x_at), whole, whole] + [whole] * 6 + [hbm] * 3,
+                  pl.BlockSpec((wide, cols), x_at), whole, whole] + [whole] * 6 + [hbm] * 3,
         out_specs=(hbm, pl.BlockSpec((cb, ffn), lambda i: (col_at(i), 0)),
-                   pl.BlockSpec((ffn, cb), lambda i: (0, col_at(i))), pl.BlockSpec((tile, qkv_w), x_at)),
+                   pl.BlockSpec((ffn, cb), lambda i: (0, col_at(i))), pl.BlockSpec((wide, qkv_w), x_at)),
         scratch_shapes=[VMEM((rows, ffn), BF16), VMEM((rows, ffn), BF16), VMEM((qkv_w, cols), BF16), VMEM((1, cols), F32),
                         pltpu.SemaphoreType.DMA((3,))] + comm.scratch()
         + [VMEM((tile, ffn), F32), VMEM((tile, ffn), F32), VMEM((rows, cb), BF16)],
@@ -569,18 +573,21 @@
     comm = Comm(n, rows, cols)
     tile = comm.half
     per_mb = seq // tile
-    n_seq = 2 * per_mb * mbs
-    cb = 256
+    wide = 2 * tile
+    lead = seq // wide
+    span = lead + per_mb
+    n_seq = span * mbs
+    cb = 512
     n_cols = cols // cb
     grid = n_seq + n_cols
     points = []
     for b in range(mbs):
-        points += [(0.0, []), (0.8, []), (0.0, [])] * per_mb
+        points += [(0.0, []), (1.4, []), (0.0, [])] * lead
         for j in range(per_mb - 1, -1, -1):
             s = b * (per_mb // 2) + j // 2
             points += [(1.0, []), (0.9, []), (1.45, [(s, 'pair'), (s, 'own')] if j % 2 == 0 else [])]
     for i in range(n_cols):
-        points += [(0.7, []), (1.0, []), (0.4, [])]
+        points += [(1.4, []), (2.0, []), (0.7, [])]
     points[0] = (5.5, [])
     plans = comm.tuned(ATT_PLAN, points)
 
@@ -591,13 +598,16 @@
         full, own = comm.full, comm.own
 
         def ticks(steps, k):
-            for step in steps:
-                todo = plans[step * 3 + k]
-                if todo:
-                    @pl.when(i == step)
-                    def _():
-                        for name, s in todo:
-                            getattr(comm, name)(s)
+            if any(plans[step * 3 + k] for step in steps):
+                @pl.when(jnp.logical_and(i >= steps[0], i <= steps[-1]))
+                def _():
+                    for step in steps:
+                        todo = plans[step * 3 + k]
+                        if todo:
+                            @pl.when(i == step)
+                            def _():
+                                for name, s in todo:
+                                    getattr(comm, name)(s)
 
         @pl.when(i == 0)
         def _():
@@ -614,19 +624,18 @@
             for load in loads:
                 load.wait()
 
-        span = 2 * per_mb
         first = range(n_seq)
         rest = range(n_seq, grid)
         b = lax.div(i, span)
         at = lax.rem(i, span)
         in_seq = i < n_seq
-        loading = jnp.logical_and(in_seq, at < per_mb)
+        loading = jnp.logical_and(in_seq, at < lead)
         base = b * seq
-        trow = pl.ds(pl.multiple_of(jnp.minimum(base + at * tile, rows - tile), tile), tile)
+        trow = pl.ds(pl.multiple_of(jnp.minimum(base + at * wide, rows - wide), wide), wide)
 
         def variants(fn):
             for j in range(per_mb):
-                @pl.when(jnp.logical_and(in_seq, at == 2 * per_mb - 1 - j))
+                @pl.when(jnp.logical_and(in_seq, at == span - 1 - j))
                 def _():
                     fn(j)
 
@@ -712,7 +721,7 @@
 
     def tile_map(i):
         ii = jnp.minimum(i, n_seq - 1)
-        return lax.div(ii, 2 * per_mb) * per_mb + jnp.minimum(lax.rem(ii, 2 * per_mb), per_mb - 1), 0
+        return lax.div(ii, span) * lead + jnp.minimum(lax.rem(ii, span), lead - 1), 0
 
     def col_at(i):
         return jnp.maximum(i - n_seq, 0)
@@ -724,7 +733,7 @@
         grid=(grid,),
         out_shape=(jax.ShapeDtypeStruct((rows, cols), BF16), jax.ShapeDtypeStruct((qkv_w, cols), BF16),
                    jax.ShapeDtypeStruct((hd, cols), BF16)),
-        in_specs=[pl.BlockSpec((tile, cols), tile_map),
+        in_specs=[pl.BlockSpec((wide, cols), tile_map),
                   pl.BlockSpec((rows, cb), lambda i: (0, col_at(i))), pl.BlockSpec((rows, cb), lambda i: (0, col_at(i))),
                   whole, hbm, hbm, whole, whole, whole, hbm, hbm],
         out_specs=(hbm, pl.BlockSpec((qkv_w, cb), lambda i: (0, col_at(i))),

time: 233 us -> 228 us (0.979)
  Pallas kernels: 232 us -> 227 us
    pallas_call x1, Pallas kernels: 113 us -> 108 us  [mlp_stage(): pl.pallas_call(wrapped, grid=(grid,), out_shape=(jax.ShapeDtypeStruct((ro...]
where the time goes in v4:
time: 228 us
  Pallas kernels  227 us (100%)
    pallas_call x1, Pallas kernels, mlp_stage(): pl.pallas_call(wrapped, grid=(grid,), out_shape=(jax.ShapeDtypeStruct((ro...  108 us
    pallas_call x1, Pallas kernels, attention_stage(): pl.pallas_call(kernel, grid=(grid,), out_shape=(jax.ShapeDtypeStruct((row...  105 us
    pallas_call x1, Pallas kernels, spread_copy(): pl.pallas_call(kernel, out_shape=outs, in_specs=[hbm] * 5, out_specs=[hbm...  13.9 us

profile of v4, /device:TPU:97, one launch (start us, length us, event | category | flops | bytes accessed | tf_op | source)
XLA Modules:
  0.0 227.5 jit_solution(9653479040632343220)
XLA Ops:
  0.6 108.0 %mlp_stage.1 = (bf16[2048,3072]{1,0:T(8,128)(2,1)}, bf16[3072,384]{1,0:T(8,128)(2,1)}, bf16[384,3072]{1,0:T(8,128)(2,1)}, bf16[2048,384]{1,0:T(8,128)(2,1)}) custom-call(bf16[2048,3072]{1,0:T(8,128)(2,1)} %bitcast.12, bf16[2048,3072]{1,0:T(8,128)(2,1)} %bitcast.15, bf16[2048,3072]{1,0:T(8,128)(2,1)} %bitcast.13, bf16[2048,3072]{1,0:T(8,128)(2,1)} %bitcast.16, ...), custom_call_target="tpu_custom_call" | custom-call | tf_op jit(solution)/shard_map/mlp_stage/pallas_call | solution.py:548
  108.6 104.8 %attention_stage.1 = (bf16[2048,3072]{1,0:T(8,128)(2,1)}, bf16[384,3072]{1,0:T(8,128)(2,1)}, bf16[128,3072]{1,0:T(8,128)(2,1)}) custom-call(bf16[2048,3072]{1,0:T(8,128)(2,1)} %get-tuple-element.17.dh_tile.dh_col.dh_all, bf16[2048,3072]{1,0:T(8,128)(2,1)} %bitcast.19, bf16[2048,3072]{1,0:T(8,128)(2,1)} %get-tuple-element.17.dh_tile.dh_col.dh_all, ...), custom_call_target="tpu_custom_call" | custom-call | tf_op jit(solution)/shard_map/attention_stage/pallas_call | solution.py:731
  213.5 13.9 %spread_copy.1 = (bf16[2048,3072]{1,0:T(8,128)(2,1)}, bf16[3072,384]{1,0:T(8,128)(2,1)}, bf16[384,3072]{1,0:T(8,128)(2,1)}, bf16[288,3072]{1,0:T(8,128)(2,1)}, bf16[96,3072]{1,0:T(8,128)(2,1)}) custom-call(bf16[2048,3072]{1,0:T(8,128)(2,1)} %get-tuple-element.19.refs_0_, bf16[3072,384]{1,0:T(8,128)(2,1)} %get-tuple-element.20.refs_1_, ...), custom_call_target="tpu_custom_call" | custom-call | tf_op jit(solution)/shard_map/spread_copy/pallas_call | solution.py:781

commit v5 on v4

--- a/solution.py
+++ b/solution.py
@@ -395,10 +395,10 @@
     512, 769, 964, 1029, 1154, 1352, 1417, 1414, 1549, 1539, 1674, 1799, 1934, 1932, 1937, 1995, 2002, 2064,
     2127, 2133, 2198, 2196, 2195, 2265, 2330, 2653, 2647, 2712, 2846, 2907, 3170, 3169, 3164, 3295, 3365,
     3488, 3494, 3555, 3684, 3751])
-ATT_PLAN = (54, [
-    1153, 1605, 1664, 1865, 1860, 2061, 2051, 2248, 2247, 2257, 2380, 2370, 2517, 2502, 2507, 2576, 2634,
-    2639, 2649, 2766, 2771, 2836, 2845, 2834, 2903, 2904, 2977, 3030, 3035, 3098, 3167, 3228, 3294, 3363,
-    3424, 3426, 3429, 3428, 3431, 3430])
+ATT_PLAN = (60, [
+    1089, 1605, 1664, 1865, 1860, 2061, 2051, 2257, 2248, 2247, 2389, 2380, 2370, 2512, 2571, 2566, 2703,
+    2708, 2713, 2771, 2762, 2840, 3022, 3037, 3218, 3223, 3228, 3297, 3286, 3291, 3424, 3418, 3429, 3551,
+    3620, 3678, 3683, 3746, 3751, 3814])
 VMEM_LIMIT = 64 * 1024 * 1024 - 64 * 1024
 
 
@@ -577,7 +577,7 @@
     lead = seq // wide
     span = lead + per_mb
     n_seq = span * mbs
-    cb = 512
+    cb = 384
     n_cols = cols // cb
     grid = n_seq + n_cols
     points = []
@@ -587,7 +587,7 @@
             s = b * (per_mb // 2) + j // 2
             points += [(1.0, []), (0.9, []), (1.45, [(s, 'pair'), (s, 'own')] if j % 2 == 0 else [])]
     for i in range(n_cols):
-        points += [(1.4, []), (2.0, []), (0.7, [])]
+        points += [(1.05, []), (1.5, []), (0.55, [])]
     points[0] = (5.5, [])
     plans = comm.tuned(ATT_PLAN, points)
 
@@ -731,7 +731,7 @@
     return pl.pallas_call(
         kernel,
         grid=(grid,),
-        out_shape=(jax.ShapeDtypeStruct((rows, cols), BF16), jax.ShapeDtypeStruct((qkv_w, cols), BF16),
+        out_shape=(VMEM((rows, cols), BF16), jax.ShapeDtypeStruct((qkv_w, cols), BF16),
                    jax.ShapeDtypeStruct((hd, cols), BF16)),
         in_specs=[pl.BlockSpec((wide, cols), tile_map),
                   pl.BlockSpec((rows, cb), lambda i: (0, col_at(i))), pl.BlockSpec((rows, cb), lambda i: (0, col_at(i))),
@@ -742,7 +742,7 @@
                         VMEM((rows, qkv_w), BF16), VMEM((seq, hd), F32), VMEM((seq, hd), F32), VMEM((rows, cb), BF16),
                         VMEM((tile, seq), F32), VMEM((qkv_w, cols), BF16), VMEM((hd, cols), BF16),
                         pltpu.SemaphoreType.DMA((4,))] + comm.scratch(),
-        compiler_params=pltpu.CompilerParams(collective_id=cid, has_side_effects=True, vmem_limit_bytes=VMEM_LIMIT,
+        compiler_params=pltpu.CompilerParams(collective_id=cid, has_side_effects=True, vmem_limit_bytes=VMEM_LIMIT - rows * cols * 2 - 256 * 1024,
                                              dimension_semantics=('arbitrary',)),
         name='attention_stage',
     )(dh1, x, dh1, qkv_all, w_qkv, w_out, *stats, gain, x, dh1)
@@ -761,18 +761,20 @@
     total = sum(len(mv) for mv in moves)
 
     def kernel(*refs):
-        ins, dsts, bufs, (in_sem, out_sem) = refs[:5], refs[5:10], refs[10:15], refs[15:]
+        ins, dsts, bufs, (in_sem, out_sem) = refs[:5], refs[5:10], (refs[0],) + refs[10:14], refs[14:]
         reads, writes = [], []
         for a, mv in enumerate(moves):
             for frm, to, size in mv:
                 k = len(reads)
                 here = bufs[a].at[pl.ds(to, size), :]
-                reads.append(pltpu.make_async_copy(ins[a].at[pl.ds(frm, size), :], here, in_sem.at[k]))
+                reads.append(pltpu.make_async_copy(ins[a].at[pl.ds(frm, size), :], here, in_sem.at[k]) if a else None)
                 writes.append(pltpu.make_async_copy(here, dsts[a].at[pl.ds(to, size), :], out_sem.at[k]))
         for read in reads:
-            read.start()
+            if read is not None:
+                read.start()
         for read, write in zip(reads, writes):
-            read.wait()
+            if read is not None:
+                read.wait()
             write.start()
         for write in writes:
             write.wait()
@@ -781,11 +783,11 @@
     return pl.pallas_call(
         kernel,
         out_shape=outs,
-        in_specs=[hbm] * 5,
+        in_specs=[pl.BlockSpec(memory_space=VMEM)] + [hbm] * 4,
         out_specs=[hbm] * 5,
-        scratch_shapes=[VMEM(o.shape, o.dtype) for o in outs]
+        scratch_shapes=[VMEM(o.shape, o.dtype) for o in outs[1:]]
         + [pltpu.SemaphoreType.DMA((total,)), pltpu.SemaphoreType.DMA((total,))],
-        compiler_params=pltpu.CompilerParams(vmem_limit_bytes=VMEM_LIMIT),
+        compiler_params=pltpu.CompilerParams(vmem_limit_bytes=32 * 1024 * 1024),
         name='spread_copy',
     )(*srcs)
 

time: 228 us -> 228 us (level)
  local copies, waits for them, and re-layouts: 0 us -> 6.12 us
  Pallas kernels: 227 us -> 221 us
    unnamed x0 -> x8, local copies, waits for them, and re-layouts: none -> 6.12 us
    pallas_call x2, Pallas kernels: 119 us -> 113 us  [the longest x1 105 us: attention_stage(): pl.pallas_call(kernel, grid=(grid,), out_shape=(VMEM((rows, cols), BF16),...]
where the time goes in v5:
time: 228 us
  Pallas kernels  221 us (97%)
  local copies, waits for them, and re-layouts  6.12 us (3%)
    pallas_call x1, Pallas kernels, mlp_stage(): pl.pallas_call(wrapped, grid=(grid,), out_shape=(jax.ShapeDtypeStruct((ro...  108 us
    pallas_call x1, Pallas kernels, attention_stage(): pl.pallas_call(kernel, grid=(grid,), out_shape=(VMEM((rows, cols), BF16),...  105 us
    pallas_call x1, Pallas kernels, spread_copy(): pl.pallas_call(kernel, out_shape=outs, in_specs=[pl.BlockSpec(memory_spac...  8.4 us
    unnamed x8, local copies, waits for them, and re-layouts  6.12 us

profile of v5, /device:TPU:97, one launch (start us, length us, event | category | flops | bytes accessed | tf_op | source)
XLA Modules:
  0.0 227.8 jit_solution(7229704360848764181)
XLA Ops:
  0.6 107.9 %mlp_stage.1 = (bf16[2048,3072]{1,0:T(8,128)(2,1)}, bf16[3072,384]{1,0:T(8,128)(2,1)}, bf16[384,3072]{1,0:T(8,128)(2,1)}, bf16[2048,384]{1,0:T(8,128)(2,1)}) custom-call(bf16[2048,3072]{1,0:T(8,128)(2,1)} %bitcast.12, bf16[2048,3072]{1,0:T(8,128)(2,1)} %bitcast.15, bf16[2048,3072]{1,0:T(8,128)(2,1)} %bitcast.13, bf16[2048,3072]{1,0:T(8,128)(2,1)} %bitcast.16, ...), custom_call_target="tpu_custom_call" | custom-call | tf_op jit(solution)/shard_map/mlp_stage/pallas_call | solution.py:548
  108.6 104.5 %attention_stage.1 = (bf16[2048,3072]{1,0:T(8,128)(2,1)S(1)}, bf16[384,3072]{1,0:T(8,128)(2,1)}, bf16[128,3072]{1,0:T(8,128)(2,1)}) custom-call(bf16[2048,3072]{1,0:T(8,128)(2,1)} %get-tuple-element.17.dh_tile.dh_col.dh_all, bf16[2048,3072]{1,0:T(8,128)(2,1)} %bitcast.19, bf16[2048,3072]{1,0:T(8,128)(2,1)} %get-tuple-element.17.dh_tile.dh_col.dh_all, ...), custom_call_target="tpu_custom_call" | custom-call | tf_op jit(solution)/shard_map/attention_stage/pallas_call | solution.py:731
  213.1 0.0 copy-start
  213.1 1.7 copy-done
  214.8 0.0 copy-start.1
  214.8 1.7 copy-done.1
  216.5 0.0 copy-start.2
  216.5 1.7 copy-done.2
  218.1 0.0 copy-start.3
  218.1 1.1 copy-done.3
  219.3 8.4 %spread_copy.1 = (bf16[2048,3072]{1,0:T(8,128)(2,1)}, bf16[3072,384]{1,0:T(8,128)(2,1)}, bf16[384,3072]{1,0:T(8,128)(2,1)}, bf16[288,3072]{1,0:T(8,128)(2,1)}, bf16[96,3072]{1,0:T(8,128)(2,1)}) custom-call(bf16[2048,3072]{1,0:T(8,128)(2,1)S(1)} %get-tuple-element.19.refs_0_, bf16[3072,384]{1,0:T(8,128)(2,1)S(1)} %copy-done, bf16[384,3072]{1,0:T(8,128)(2,1)S(1)} %copy-done.1, ...), custom_call_target="tpu_custom_call" | custom-call | tf_op jit(solution)/shard_map/spread_copy/pallas_call | solution.py:783
Async XLA Ops:
  213.1 1.7 copy-start
  214.8 1.7 copy-start.1
  216.5 1.7 copy-start.2
  218.1 1.1 copy-start.3
